TPU v7x, 32 devices: a whole 2x2x4 slice. The times are simulated.
32 devices in a mesh: part: 2 (over x), row: 4 (over z), col: 4 (over y, core).
Axes of the slice: x: 2, y: 2, z: 4, core: 2. Of those that a mesh axis runs over, the one named last changes fastest.
Arguments:
- ratings: float32 [1024, 32768], P(('part', 'row'), 'col'), parts along dimension 0
- mask: int32 [1024, 32768], P(('part', 'row'), 'col'), parts along dimension 0
- user_init: float32 [1024, 64], P(('part', 'row')), parts along dimension 0
- item_init: float32 [65536, 64], P(('part', 'col')), parts along dimension 0
Outputs:
- output 1: float32 [1024, 64], P(('part', 'row')), parts along dimension 0
- output 2: float32 [65536, 64], P(('part', 'col')), parts along dimension 0
There are 2 independent parts. A program takes and returns all parts, laid end to end along the dimension named above; each array names one.
All inputs are finite; a program needn't handle non-finite values.
Results may differ from a plain program's by a relative error of at most 0.00388836.
Values are sent between devices in bfloat16 or wider.
A program may use at most 1 GiB of HBM per device.

v0:
```python
import jax
import jax.numpy as jnp
from jax import lax
from jax.sharding import PartitionSpec as P

CG_STEPS = 4
RIDGE_WEIGHT = 0.0005


def obs_scores(fixed_bf, moving_bf, by_rows):
    if by_rows:
        return lax.dot_general(moving_bf, fixed_bf, (((1,), (1,)), ((), ())), preferred_element_type=jnp.float32)
    return lax.dot_general(fixed_bf, moving_bf, (((1,), (1,)), ((), ())), preferred_element_type=jnp.float32)


def back_product(block_bf, fixed_bf, by_rows):
    contract = 1 if by_rows else 0
    return lax.dot_general(block_bf, fixed_bf, (((contract,), (0,)), ((), ())), preferred_element_type=jnp.float32)


def cg_block(mask_on, ratings_blk, fixed_fac, start, ridge, axis_name, by_rows):
    fixed_bf = fixed_fac.astype(jnp.bfloat16)
    scores = obs_scores(fixed_bf, start.astype(jnp.bfloat16), by_rows)
    resid_obs = jnp.where(mask_on, ratings_blk - scores, 0.0).astype(jnp.bfloat16)
    residual = lax.psum(back_product(resid_obs, fixed_bf, by_rows), axis_name) - ridge * start
    direction = residual
    estimate = start
    res_sq = jnp.sum(residual * residual, axis=1, keepdims=True)
    for cg_step in range(CG_STEPS):
        scores = obs_scores(fixed_bf, direction.astype(jnp.bfloat16), by_rows)
        masked = jnp.where(mask_on, scores.astype(jnp.bfloat16), 0.0)
        gram_dir = lax.psum(back_product(masked, fixed_bf, by_rows), axis_name) + ridge * direction
        step_size = res_sq / jnp.sum(direction * gram_dir, axis=1, keepdims=True)
        estimate = estimate + step_size * direction
        if cg_step + 1 < CG_STEPS:
            residual = residual - step_size * gram_dir
            new_sq = jnp.sum(residual * residual, axis=1, keepdims=True)
            direction = residual + (new_sq / res_sq) * direction
            res_sq = new_sq
    return estimate


def solution(mesh):
    row_size = mesh.shape["row"]
    col_size = mesh.shape["col"]
    grid_spec = P(("part", "row"), "col")
    user_spec = P(("part", "row"), None)
    item_spec = P(("part", "col"), None)

    def local_step(ratings_blk, mask_blk, user_blk, item_blk):
        users_part = ratings_blk.shape[0] * row_size
        items_part = ratings_blk.shape[1] * col_size
        mask_on = mask_blk > 0
        user_new = cg_block(mask_on, ratings_blk, item_blk, user_blk, RIDGE_WEIGHT * items_part, "col", True)
        item_new = cg_block(mask_on, ratings_blk, user_new, item_blk, RIDGE_WEIGHT * users_part, "row", False)
        return user_new, item_new

    return jax.shard_map(local_step, mesh=mesh, in_specs=(grid_spec, grid_spec, user_spec, item_spec), out_specs=(user_spec, item_spec), check_vma=False)
```

profile of v0, /device:TPU:0, one launch (start us, length us, event | category | flops | bytes accessed | tf_op | source)
XLA Modules:
  0.0 558.6 jit_solution(5391861551752157692)
XLA Ops:
  7.2 0.0 all-reduce.6.cloned.1.call-start
  7.2 0.0 copy-start.7
  7.2 2.9 broadcast_compare_fusion
  10.1 0.0 copy-done.7
  10.1 0.0 copy-start.10
  10.1 0.1 convert_element_type.74
  10.2 0.6 copy-done.10
  10.9 3.7 fusion.21
  14.6 13.0 %psum.70 = f32[128,64]{0,1:T(8,128)S(1)} all-reduce(f32[128,64]{0,1:T(8,128)S(1)} %fusion.21), channel_id=1, replica_groups=mesh['part'=2,'row'=4,'col'=4] {'col'}, use_global_device_ids=true, to_apply=%region_0.1 | all-reduce | flops 8192 | bytes 65536 | tf_op jit(solution)/shard_map/psum | solution.py:25
  27.6 1.5 fusion.20
  29.1 10.3 %psum.71 = f32[128,64]{0,1:T(8,128)S(1)} all-reduce(f32[128,64]{0,1:T(8,128)S(1)} %fusion.20), channel_id=1, replica_groups=mesh['part'=2,'row'=4,'col'=4] {'col'}, use_global_device_ids=true, to_apply=%region_2.3 | all-reduce | flops 8192 | bytes 65536 | tf_op jit(solution)/shard_map/psum | solution.py:32
  39.5 1.6 fusion.19
  41.1 10.3 %psum.72 = f32[128,64]{0,1:T(8,128)S(1)} all-reduce(f32[128,64]{0,1:T(8,128)S(1)} %fusion.19), channel_id=1, replica_groups=mesh['part'=2,'row'=4,'col'=4] {'col'}, use_global_device_ids=true, to_apply=%region_5.6 | all-reduce | flops 8192 | bytes 65536 | tf_op jit(solution)/shard_map/psum | solution.py:32
  51.4 1.5 fusion.18
  53.0 10.3 %psum.73 = f32[128,64]{0,1:T(8,128)S(1)} all-reduce(f32[128,64]{0,1:T(8,128)S(1)} %fusion.18), channel_id=1, replica_groups=mesh['part'=2,'row'=4,'col'=4] {'col'}, use_global_device_ids=true, to_apply=%region_8.9 | all-reduce | flops 8192 | bytes 65536 | tf_op jit(solution)/shard_map/psum | solution.py:32
  63.4 1.5 fusion.17
  64.9 10.7 %psum.74 = f32[128,64]{0,1:T(8,128)S(1)} all-reduce(f32[128,64]{0,1:T(8,128)S(1)} %fusion.17), channel_id=1, replica_groups=mesh['part'=2,'row'=4,'col'=4] {'col'}, use_global_device_ids=true, to_apply=%region_11.12 | all-reduce | flops 8192 | bytes 65536 | tf_op jit(solution)/shard_map/psum | solution.py:32
  75.6 0.6 fusion.58
  76.3 4.7 fusion.16
  81.0 0.0 all-reduce.6.cloned.1.call-update
  81.0 0.0 all-reduce.8.cloned.1.call-start
  81.1 86.3 %all-reduce.6.cloned.1.call-done = f32[8192,64]{0,1:T(8,128)} async-done(((f32[8192,64]{0,1:T(8,128)}), f32[8192,64]{0,1:T(8,128)}) %all-reduce.6.cloned.1.call-update) | async-done | bytes 2097168 | tf_op jit(solution)/shard_map/psum | solution.py:25
  167.4 2.5 multiply_subtract_fusion.3
  169.8 2.7 fusion.15
  172.5 0.0 all-reduce.8.cloned.1.call-update
  172.5 0.2 all-reduce.10.cloned.1.call-start
  172.8 84.9 %all-reduce.8.cloned.1.call-done = f32[8192,64]{0,1:T(8,128)} async-done(((f32[8192,64]{0,1:T(8,128)}), f32[8192,64]{0,1:T(8,128)}) %all-reduce.8.cloned.1.call-update) | async-done | bytes 2097168 | tf_op jit(solution)/shard_map/psum | solution.py:32
  257.7 0.0 copy-start
  257.7 2.3 multiply_reduce_fusion.6
  260.0 0.0 copy-done
  260.0 0.5 multiply_reduce_fusion.5
  260.5 4.3 fusion.14
  264.8 0.0 all-reduce.10.cloned.1.call-update
  264.8 0.0 all-reduce.12.cloned.1.call-start
  264.9 85.1 %all-reduce.10.cloned.1.call-done = f32[8192,64]{0,1:T(8,128)} async-done(((f32[8192,64]{0,1:T(8,128)}), f32[8192,64]{0,1:T(8,128)}) %all-reduce.10.cloned.1.call-update) | async-done | bytes 2097168 | tf_op jit(solution)/shard_map/psum | solution.py:32
  350.0 0.0 copy-start.1
  350.0 0.0 copy-start.9
  350.0 3.1 multiply_reduce_fusion.4
  353.1 0.0 copy-done.1
  353.1 0.3 copy-done.9
  353.5 0.9 multiply_reduce_fusion.3
  354.4 0.0 copy-start.5
  354.4 1.3 copy-done.5
  355.7 1.9 multiply_add_fusion.3
  357.5 4.3 fusion.13
  361.8 0.0 all-reduce.12.cloned.1.call-update
  361.8 0.0 all-reduce.14.cloned.1.call-start
  361.9 85.1 %all-reduce.12.cloned.1.call-done = f32[8192,64]{0,1:T(8,128)} async-done(((f32[8192,64]{0,1:T(8,128)}), f32[8192,64]{0,1:T(8,128)}) %all-reduce.12.cloned.1.call-update) | async-done | bytes 2097168 | tf_op jit(solution)/shard_map/psum | solution.py:32
  447.0 0.0 copy-start.3
  447.0 0.0 copy-start.6
  447.0 2.7 multiply_reduce_fusion.2
  449.8 0.1 copy-done.3
  449.9 0.6 copy-done.6
  450.5 0.0 copy-start.8
  450.5 2.3 multiply_reduce_fusion.1
  452.8 0.0 copy-done.8
  452.8 1.7 multiply_add_fusion.1
  454.5 4.3 fusion.12
  458.8 0.0 all-reduce.14.cloned.1.call-update
  458.8 85.2 %all-reduce.14.cloned.1.call-done = f32[8192,64]{0,1:T(8,128)} async-done(((f32[8192,64]{0,1:T(8,128)}), f32[8192,64]{0,1:T(8,128)}) %all-reduce.14.cloned.1.call-update) | async-done | bytes 2097168 | tf_op jit(solution)/shard_map/psum | solution.py:32
  544.0 2.7 multiply_reduce_fusion
  546.7 0.1 copy-done.2
  546.8 0.6 copy-done.4
  547.5 4.6 multiply_add_fusion
  (26 shorter events, 0.4 us)
Async XLA Ops:
  7.2 160.2 %all-reduce.6.cloned.1.call-start = ((), (), s32[]{:S(2)}) async-start(), calls=%async_computation | async-start | bytes 4194304 | tf_op jit(solution)/shard_map/psum | solution.py:25
  7.2 2.9 copy-start.7
  10.1 0.8 copy-start.10
  81.0 176.7 %all-reduce.8.cloned.1.call-start = ((), (), s32[]{:S(2)}) async-start(), calls=%async_computation.1 | async-start | bytes 4194304 | tf_op jit(solution)/shard_map/psum | solution.py:32
  172.5 177.5 %all-reduce.10.cloned.1.call-start = ((), (), s32[]{:S(2)}) async-start(), calls=%async_computation.2 | async-start | bytes 4194304 | tf_op jit(solution)/shard_map/psum | solution.py:32
  257.7 2.3 copy-start
  264.8 182.2 %all-reduce.12.cloned.1.call-start = ((), (), s32[]{:S(2)}) async-start(), calls=%async_computation.3 | async-start | bytes 4194304 | tf_op jit(solution)/shard_map/psum | solution.py:32
  350.0 3.1 copy-start.1
  350.0 3.5 copy-start.9
  354.4 1.3 copy-start.5
  361.8 182.2 %all-reduce.14.cloned.1.call-start = ((), (), s32[]{:S(2)}) async-start(), calls=%async_computation.4 | async-start | bytes 4194304 | tf_op jit(solution)/shard_map/psum | solution.py:32
  447.0 2.9 copy-start.3
  447.0 3.5 copy-start.6
  450.5 2.3 copy-start.8
  544.0 2.9 copy-start.2
  544.0 3.5 copy-start.4
Sparse Core Ops, SparseCore 0:
  81.2 86.1 all-reduce.5
  172.7 85.0 all-reduce.7
  264.9 85.0 all-reduce.9
  362.0 85.0 all-reduce.11
  458.9 85.0 all-reduce.13
where the time goes:
time: 559 us
  waiting for transfers between devices  427 us (76%)
  blocking collectives  54.4 us (10%)
  matrix products  30.2 us (5%)
  other arithmetic  29.1 us (5%)
  between operations  14 us (3%)
    psum x4, waiting for transfers between devices, cg_block(): lax.psum(back_product(masked, fixed_bf, by_rows), axis_name)  340 us
    psum x1, waiting for transfers between devices, cg_block(): lax.psum(back_product(resid_obs, fixed_bf, by_rows), axis_name)  86.3 us
    psum x4, blocking collectives, cg_block(): lax.psum(back_product(masked, fixed_bf, by_rows), axis_name)  41.5 us
    dot_general x10, matrix products, back_product(): lax.dot_general(block_bf, fixed_bf, (((contract,), (0,)), ((), ())), pref...  30.2 us
    psum x1, blocking collectives, cg_block(): lax.psum(back_product(resid_obs, fixed_bf, by_rows), axis_name)  13 us
  transfers between devices with their start and end apart: 5, of which 5 were waited for; matrix products, arithmetic and copies ran while one was open for 0% of the time, Pallas kernels for 0%

commit v1 on v0

v1 whole, which is shorter than its diff:
```python
import jax
import jax.numpy as jnp
from jax import lax
from jax.sharding import PartitionSpec as P

CG_STEPS = 4
RIDGE_WEIGHT = 0.0005
BF, F32 = jnp.bfloat16, jnp.float32


def mm(a, b, dims):
    return lax.dot_general(a, b, (dims, ((), ())), preferred_element_type=F32)


def cg_steps(apply_a, start, residual, axis):
    direction = residual
    estimate = start
    res_sq = jnp.sum(residual * residual, axis=axis, keepdims=True)
    for cg_step in range(CG_STEPS):
        gram_dir = apply_a(direction)
        step_size = res_sq / jnp.sum(direction * gram_dir, axis=axis, keepdims=True)
        estimate = estimate + step_size * direction
        if cg_step + 1 < CG_STEPS:
            residual = residual - step_size * gram_dir
            new_sq = jnp.sum(residual * residual, axis=axis, keepdims=True)
            direction = residual + (new_sq / res_sq) * direction
            res_sq = new_sq
    return estimate


def solution(mesh):
    row_size = mesh.shape["row"]
    col_size = mesh.shape["col"]
    grid_spec = P(("part", "row"), "col")
    user_spec = P(("part", "row"), None)
    item_spec = P(("part", "col"), None)

    def local_step(ratings, mask, user_blk, item_blk):
        users_part = ratings.shape[0] * row_size
        items_part = ratings.shape[1] * col_size
        items_own = ratings.shape[1] // row_size
        mask_on = mask > 0
        mask_bf = mask_on.astype(BF)
        mask_item = lax.all_to_all(mask_bf, "row", split_axis=1, concat_axis=0, tiled=True)
        user_t, item_t = user_blk.T, item_blk.T

        item_bf = item_t.astype(BF)
        ridge = RIDGE_WEIGHT * items_part
        scores = mm(user_t.astype(BF), item_bf, ((0,), (0,)))
        obs = jnp.where(mask_on, ratings - scores, 0.0).astype(BF)
        residual = lax.psum(mm(item_bf, obs, ((1,), (1,))), "col") - ridge * user_t

        def apply_user(x):
            scores = mm(x.astype(BF), item_bf, ((0,), (0,)))
            masked = mask_bf * scores.astype(BF)
            return lax.psum(mm(item_bf, masked, ((1,), (1,))), "col") + ridge * x

        user_new = cg_steps(apply_user, user_t, residual, 0)

        ridge_i = RIDGE_WEIGHT * users_part
        own_bf = user_new.astype(BF)
        all_bf = lax.all_gather(own_bf, "row", axis=1, tiled=True)
        scores = mm(own_bf, item_bf, ((0,), (0,)))
        obs = jnp.where(mask_on, ratings - scores, 0.0).astype(BF)
        part = mm(own_bf, obs, ((1,), (0,)))
        start = lax.dynamic_slice_in_dim(item_t, lax.axis_index("row") * items_own, items_own, 1)
        residual = lax.psum_scatter(part, "row", scatter_dimension=1, tiled=True) - ridge_i * start

        def apply_item(x):
            scores = mm(all_bf, x.astype(BF), ((0,), (0,)))
            masked = mask_item * scores.astype(BF)
            return mm(all_bf, masked, ((1,), (0,))) + ridge_i * x

        item_new = cg_steps(apply_item, start, residual, 0)
        item_new = lax.all_gather(item_new, "row", axis=1, tiled=True)
        return user_new.T, item_new.T

    return jax.shard_map(local_step, mesh=mesh, in_specs=(grid_spec, grid_spec, user_spec, item_spec), out_specs=(user_spec, item_spec), check_vma=False)
```

time: 559 us -> 257 us (0.46)
  waiting for transfers between devices: 427 us -> 45.6 us
  blocking collectives: 54.4 us -> 140 us
  other arithmetic: 29.1 us -> 16.1 us
  local copies, waits for them, and re-layouts: 3.72 us -> 12.7 us
  matrix products: 30.2 us -> 23.4 us
    psum x5 -> x0, waiting for transfers between devices: 427 us -> none  [the longest x4 340 us: cg_block(): lax.psum(back_product(masked, fixed_bf, by_rows), axis_name)]
    all_gather x0 -> x1, blocking collectives: none -> 85.2 us  [local_step(): all_bf = lax.all_gather(own_bf, 'row', axis=1, tiled=True)]
    all_gather x0 -> x1, waiting for transfers between devices: none -> 45.5 us  [local_step(): item_new = lax.all_gather(item_new, 'row', axis=1, tiled=True)]
    reduce_sum x14 -> x10, other arithmetic: 14.7 us -> 3.74 us  [the longest x6 3.62 us: cg_steps(): new_sq = jnp.sum(residual * residual, axis=axis, keepdims=True)]
    dot_general x10, matrix products: 30.2 us -> 23.4 us  [mm(): return lax.dot_general(a, b, (dims, ((), ())), preferred_element_type=F32)]
  transfers between devices with their start and end apart: 5 -> 3, of which waited for: 5 -> 1; matrix products, arithmetic and copies ran while one was open for 0% -> 2% of each run, Pallas kernels for 0% -> 0%
where the time goes in v1:
time: 257 us
  blocking collectives  140 us (54%)
  waiting for transfers between devices  45.6 us (18%)
  matrix products  23.4 us (9%)
  other arithmetic  16.1 us (6%)
  between operations  14.3 us (6%)
  local copies, waits for them, and re-layouts  12.7 us (5%)
  starting transfers between devices  4.91 us (2%)
    all_gather x1, blocking collectives, local_step(): all_bf = lax.all_gather(own_bf, 'row', axis=1, tiled=True)  85.2 us
    all_gather x1, waiting for transfers between devices, local_step(): item_new = lax.all_gather(item_new, 'row', axis=1, tiled=True)  45.5 us
    psum x4, blocking collectives, apply_user(): return lax.psum(mm(item_bf, masked, ((1,), (1,))), 'col') + ridge * x  41.5 us
    dot_general x10, matrix products, mm(): return lax.dot_general(a, b, (dims, ((), ())), preferred_element_type=F32)  23.4 us
    psum x1, blocking collectives, local_step(): residual = lax.psum(mm(item_bf, obs, ((1,), (1,))), 'col') - ridge * user_t  13 us
    unnamed x11, local copies, waits for them, and re-layouts  7.4 us
    all_to_all x2, local copies, waits for them, and re-layouts, local_step(): lax.all_to_all(mask_bf, 'row', split_axis=1, concat_axis=0, tiled=True)  5.35 us
  transfers between devices with their start and end apart: 3, of which 1 were waited for; matrix products, arithmetic and copies ran while one was open for 2% of the time, Pallas kernels for 0%

profile of v1, /device:TPU:0, one launch (start us, length us, event | category | flops | bytes accessed | tf_op | source)
XLA Modules:
  0.0 256.6 jit_solution(911596404946240703)
XLA Ops:
  7.2 0.0 reduce-scatter.2.cloned.1.call-start
  7.2 1.7 convert_element_type.66
  8.9 0.0 copy-start.4
  8.9 4.3 %fusion.63 = (bf16[128,8192]{1,0:T(8,128)(2,1)}, pred[128,8192]{1,0:T(32,128)(4,1)S(1)}) fusion(s32[128,8192]{1,0:T(8,128)} %param.5), kind=kLoop, calls=%fused_computation.102 | loop fusion | flops 2097152 | bytes 7340032 | tf_op jit(solution)/shard_map/all_to_all | solution.py:44
  13.2 0.0 copy-done.4
  13.2 3.7 %fusion.20 = f32[64,128]{1,0:T(8,128)S(1)} fusion(bf16[8192,64]{0,1:T(8,128)(2,1)S(1)} %convert_element_type.66, pred[128,8192]{1,0:T(32,128)(4,1)S(1)} %get-tuple-element.11, f32[128,8192]{1,0:T(8,128)} %param.4, f32[128,64]{0,1:T(8,128)S(1)} %copy-done.4), kind=kOutput, calls=%fused_computation.35 | convolution fusion | flops 271581184 | bytes 6356992 | tf_op jit(solution)/shard_map/dot_general | solution.py:12
  16.9 13.0 %psum.35 = f32[64,128]{1,0:T(8,128)S(1)} all-reduce(f32[64,128]{1,0:T(8,128)S(1)} %fusion.20), channel_id=1, replica_groups=mesh['part'=2,'row'=4,'col'=4] {'col'}, use_global_device_ids=true, to_apply=%region_0.1 | all-reduce | flops 8192 | bytes 65536 | tf_op jit(solution)/shard_map/psum | solution.py:51
  29.9 1.5 fusion.21
  31.5 10.3 %psum.36 = f32[64,128]{1,0:T(8,128)S(1)} all-reduce(f32[64,128]{1,0:T(8,128)S(1)} %fusion.21), channel_id=1, replica_groups=mesh['part'=2,'row'=4,'col'=4] {'col'}, use_global_device_ids=true, to_apply=%region_2.3 | all-reduce | flops 8192 | bytes 65536 | tf_op jit(solution)/shard_map/psum | solution.py:56
  41.8 1.6 fusion.22
  43.4 10.3 %psum.37 = f32[64,128]{1,0:T(8,128)S(1)} all-reduce(f32[64,128]{1,0:T(8,128)S(1)} %fusion.22), channel_id=1, replica_groups=mesh['part'=2,'row'=4,'col'=4] {'col'}, use_global_device_ids=true, to_apply=%region_5.6 | all-reduce | flops 8192 | bytes 65536 | tf_op jit(solution)/shard_map/psum | solution.py:56
  53.8 1.5 fusion.23
  55.3 10.3 %psum.38 = f32[64,128]{1,0:T(8,128)S(1)} all-reduce(f32[64,128]{1,0:T(8,128)S(1)} %fusion.23), channel_id=1, replica_groups=mesh['part'=2,'row'=4,'col'=4] {'col'}, use_global_device_ids=true, to_apply=%region_8.9 | all-reduce | flops 8192 | bytes 65536 | tf_op jit(solution)/shard_map/psum | solution.py:56
  65.7 1.5 fusion.24
  67.2 10.7 %psum.39 = f32[64,128]{1,0:T(8,128)S(1)} all-reduce(f32[64,128]{1,0:T(8,128)S(1)} %fusion.24), channel_id=1, replica_groups=mesh['part'=2,'row'=4,'col'=4] {'col'}, use_global_device_ids=true, to_apply=%region_11.12 | all-reduce | flops 8192 | bytes 65536 | tf_op jit(solution)/shard_map/psum | solution.py:56
  78.0 0.6 fusion.64
  78.6 4.7 %fusion.13 = f32[64,8192]{1,0:T(8,128)} fusion(bf16[64,128]{1,0:T(8,128)(2,1)S(1)} %get-tuple-element.12, pred[128,8192]{1,0:T(32,128)(4,1)S(1)} %get-tuple-element.11, f32[128,8192]{1,0:T(8,128)} %param.4, bf16[8192,64]{0,1:T(8,128)(2,1)S(1)} %convert_element_type.66), kind=kOutput, calls=%fused_computation.28 | convolution fusion | flops 271581184 | bytes 8404992 | tf_op jit(solution)/shard_map/dot_general | solution.py:12
  83.4 0.0 copy-start
  83.4 0.0 reduce-scatter.2.cloned.1.call-update
  83.4 1.6 copy-done
  84.9 2.4 copy.6
  87.4 4.9 %all-to-all-start = ((bf16[128,4,2048]{0,2,1:T(8,128)(2,1)}), bf16[128,4,2048]{0,2,1:T(8,128)(2,1)S(1)}, u32[]{:S(2)}, u32[]{:S(2)}) async-start(bf16[128,4,2048]{0,2,1:T(8,128)(2,1)} %bitcast.67), calls=%async_computation.1 | async-start | bytes 4194304 | tf_op jit(solution)/shard_map/all_to_all | solution.py:44
  92.2 0.0 all-gather.2.cloned.1.call-start
  92.2 85.2 %all_gather.6 = bf16[64,512]{1,0:T(8,128)(2,1)S(1)} all-gather(bf16[64,128]{1,0:T(8,128)(2,1)S(1)} %get-tuple-element.12), channel_id=1, replica_groups=mesh['part'=2,'row'=4,'col'=4] {'row'}, dimensions={1}, use_global_device_ids=true | all-gather | bytes 81920 | tf_op jit(solution)/shard_map/all_gather | solution.py:62
  177.4 0.0 all-to-all-done
  177.4 0.0 copy-start.2
  177.4 1.3 copy-done.2
  178.7 2.9 %copy.7 = bf16[4,128,2048]{2,1,0:T(8,128)(2,1)S(1)} copy(bf16[4,128,2048]{1,2,0:T(8,128)(2,1)} %bitcast.66) | data formatting | bytes 4194304 | tf_op jit(solution)/shard_map/all_to_all | solution.py:44
  181.7 0.0 reduce-scatter.2.cloned.1.call-done
  181.7 1.3 fusion.29
  183.0 1.1 multiply_reduce_fusion.5
  184.1 0.0 copy-start.1
  184.1 0.1 multiply_reduce_fusion.4
  184.2 0.7 copy-done.1
  184.9 1.1 multiply_add_fusion.2
  186.0 1.9 multiply_reduce_fusion.3
  187.9 1.3 multiply_reduce_fusion.2
  189.2 0.0 copy-start.3
  189.2 0.8 copy-done.3
  190.0 0.9 multiply_add_fusion.1
  190.8 3.2 %multiply_reduce_fusion.1 = (f32[2048]{0:T(1024)S(1)}, f32[64,2048]{1,0:T(8,128)}) fusion(f32[64,2048]{1,0:T(8,128)} %multiply_add_fusion.1, bf16[64,512]{1,0:T(8,128)(2,1)S(1)} %all_gather.6, bf16[512,2048]{1,0:T(8,128)(2,1)S(1)} %bitcast.64), kind=kOutput, calls=%fused_computation.53 | convolution fusion | flops 271185920 | bytes 3219456 | tf_op jit(solution)/shard_map/dot_general | solution.py:12
  194.0 2.1 multiply_reduce_fusion
  196.1 2.6 %fusion.19 = f32[2048]{0:T(1024)S(1)} fusion(bf16[64,512]{1,0:T(8,128)(2,1)S(1)} %all_gather.6, bf16[512,2048]{1,0:T(8,128)(2,1)S(1)} %bitcast.65, f32[64,2048]{1,0:T(8,128)} %get-tuple-element.7, f32[64,2048]{1,0:T(8,128)} %multiply_add_fusion.1, f32[2048]{0:T(1024)S(1)} %div.124), kind=kOutput, calls=%fused_computation.34 | convolution fusion | flops 271710208 | bytes 3227648 | tf_op jit(solution)/shard_map/dot_general | solution.py:12
  198.8 2.4 fusion.32
  201.2 0.0 all-gather.2.cloned.1.call-update
  201.2 45.5 %all-gather.2.cloned.1.call-done = f32[64,8192]{1,0:T(8,128)} async-done(((f32[64,2048]{1,0:T(8,128)}), f32[64,8192]{1,0:T(8,128)}) %all-gather.2.cloned.1.call-update) | async-done | bytes 2097168 | tf_op jit(solution)/shard_map/all_gather | solution.py:75
  246.7 3.1 %copy.16 = f32[8192,64]{0,1:T(8,128)} copy(f32[8192,64]{0,1:T(8,128)} %bitcast.68) | data formatting | bytes 4194304
  (24 shorter events, 0.3 us)
Async XLA Ops:
  7.2 174.5 %reduce-scatter.2.cloned.1.call-start = ((), (), s32[]{:S(2)}) async-start(), calls=%async_computation.2 | async-start | bytes 2621440 | tf_op jit(solution)/shard_map/reduce_scatter | solution.py:67
  8.9 4.3 %copy-start.4 = (f32[128,64]{0,1:T(8,128)S(1)}, f32[128,64]{0,1:T(8,128)}, u32[]{:S(2)}) copy-start(f32[128,64]{0,1:T(8,128)} %param.6) | copy-start | bytes 98308
  83.4 1.6 copy-start
  87.4 90.0 %all-to-all-start = ((bf16[128,4,2048]{0,2,1:T(8,128)(2,1)}), bf16[128,4,2048]{0,2,1:T(8,128)(2,1)S(1)}, u32[]{:S(2)}, u32[]{:S(2)}) async-start(bf16[128,4,2048]{0,2,1:T(8,128)(2,1)} %bitcast.67), calls=%async_computation.1 | async-start | bytes 4194304 | tf_op jit(solution)/shard_map/all_to_all | solution.py:44
  92.2 154.5 %all-gather.2.cloned.1.call-start = ((), (), s32[]{:S(2)}) async-start(), calls=%async_computation.3 | async-start | bytes 2621440 | tf_op jit(solution)/shard_map/all_gather | solution.py:75
  177.4 1.3 copy-start.2
  184.1 0.8 copy-start.1
  189.2 0.8 copy-start.3
Sparse Core Ops, SparseCore 0:
  83.5 75.3 reduce-scatter.1
  201.3 45.3 all-gather.1

commit v2 on v0

v2 whole, which is shorter than its diff:
```python
import functools

import jax
import jax.numpy as jnp
from jax import lax
from jax.experimental import pallas as pl
from jax.experimental.pallas import tpu as pltpu
from jax.sharding import PartitionSpec as P

CG_STEPS = 4
RIDGE_WEIGHT = 0.0005
CHUNKS = 4
BF, F32 = jnp.bfloat16, jnp.float32
MESH = pl.DeviceIdType.MESH


def mm(a, b, contract_a, contract_b):
    return lax.dot_general(a, b, (((contract_a,), (contract_b,)), ((), ())), preferred_element_type=F32)


def col_sum(a, b):
    return jnp.sum(a * b, axis=0, keepdims=True)


def cg_steps(apply_a, start, residual):
    direction = residual
    estimate = start
    res_sq = col_sum(residual, residual)
    for cg_step in range(CG_STEPS):
        gram_dir = apply_a(cg_step, direction)
        step_size = res_sq / col_sum(direction, gram_dir)
        estimate = estimate + step_size * direction
        if cg_step + 1 < CG_STEPS:
            residual = residual - step_size * gram_dir
            new_sq = col_sum(residual, residual)
            direction = residual + (new_sq / res_sq) * direction
            res_sq = new_sq
    return estimate


def kernel(
    ridge_u, ridge_i,
    r_hbm, m_hbm, w0_ref, v0_hbm,
    u_out, v_out,
    mint, rbuf, v0b, fb, mown, mrecv, ar, wg, wrow, part, rec_e, rec_x, vout,
    ld_sem, ms_sem, mr_sem, as_sem, arr_sem, ws_sem, wr_sem, rs_sem, re_sem, rx_sem, ag_sem, agr_sem, out_sem,
):
    z = lax.axis_index("row")
    c = lax.axis_index("col")
    blk = mint.shape[2]
    nc, width = part.shape[1], part.shape[3]
    hi = z // 2
    is_mid = lax.rem(z + hi, 2)

    def row_of(mirrored):
        return mirrored + hi * (3 - 2 * mirrored)

    def to_row(src, dst, send, recv, row):
        return pltpu.make_async_remote_copy(
            src_ref=src, dst_ref=dst, send_sem=send, recv_sem=recv, device_id={"row": row}, device_id_type=MESH)

    order = (1 + lax.rem(z, 2), lax.rem(z + 2, 4), 3 - 3 * lax.rem(z, 2), z)

    def load(hbm, buf, kind, s):
        return pltpu.make_async_copy(
            hbm.at[:, pl.ds(pl.multiple_of(s * blk, blk), blk)], buf.at[s], ld_sem.at[kind, s])

    for s in order:
        load(m_hbm, mint, 0, s).start()
    for s in range(4):
        load(v0_hbm, v0b, 1, s).start()
    for s in range(4):
        load(r_hbm, rbuf, 2, s).start()

    barrier = pltpu.get_barrier_semaphore()
    for off in range(1, 4):
        pl.semaphore_signal(barrier, inc=1, device_id={"row": lax.rem(z + off, 4)}, device_id_type=MESH)
        pl.semaphore_signal(barrier, inc=1, device_id={"col": lax.rem(c + off, 4)}, device_id_type=MESH)
    pl.semaphore_wait(barrier, 6)

    for j, s in enumerate(order):
        load(m_hbm, mint, 0, s).wait()
        for k in range(nc):
            m = mint[s, :, k * width:(k + 1) * width].astype(F32).astype(BF)
            mown[s, k] = m
            if j == 3:
                mrecv[z, k] = m
        if j < 3:
            to_row(mown.at[s], mrecv.at[z], ms_sem.at[s], mr_sem.at[z], s).start()

    for s in range(4):
        load(v0_hbm, v0b, 1, s).wait()
        fb[s] = v0b[s].astype(BF)
    for s in range(4):
        load(r_hbm, rbuf, 2, s).wait()

    def observed(s, k, scores):
        cols = slice(k * width, (k + 1) * width)
        return jnp.where(mint[s, :, cols] > 0, rbuf[s, :, cols] - scores, 0.0).astype(BF)

    def user_product(x, residual):
        rows = x.T.astype(BF)

        def block(s, acc):
            for k in range(nc):
                f = fb[s, :, k * width:(k + 1) * width]
                scores = mm(rows, f, 1, 0)
                masked = observed(s, k, scores) if residual else mown[s, k] * scores.astype(BF)
                acc = acc + mm(f, masked, 1, 1)
            return acc

        return lax.fori_loop(0, 4, block, jnp.zeros(x.shape, F32))

    def to_col(rnd, off):
        peer = lax.rem(c + off, 4)
        return pltpu.make_async_remote_copy(
            src_ref=ar.at[rnd, c], dst_ref=ar.at[rnd, c], send_sem=as_sem.at[rnd, off], recv_sem=arr_sem.at[rnd, c],
            device_id={"col": peer}, device_id_type=MESH)

    def from_col(rnd, off):
        peer = lax.rem(c + off, 4)
        return pltpu.make_async_remote_copy(
            src_ref=ar.at[rnd, peer], dst_ref=ar.at[rnd, peer], send_sem=as_sem.at[rnd, off],
            recv_sem=arr_sem.at[rnd, peer], device_id={"col": peer}, device_id_type=MESH)

    def sum_cols(rnd, x):
        ar[rnd, c] = x
        for off in range(1, 4):
            to_col(rnd, off).start()
        for off in range(1, 4):
            from_col(rnd, off).wait_recv()
        return (ar[rnd, 0] + ar[rnd, 1]) + (ar[rnd, 2] + ar[rnd, 3])

    w0 = w0_ref[...]
    res = sum_cols(0, user_product(w0, True)) - ridge_u * w0
    w1 = cg_steps(lambda i, p: sum_cols(i + 1, user_product(p, False)) + ridge_u * p, w0, res)
    u_out[...] = w1

    wg[z] = w1.astype(BF)
    for off in range(1, 4):
        peer = lax.rem(z + off, 4)
        to_row(wg.at[z], wg.at[z], ws_sem.at[peer], wr_sem.at[z], peer).start()

    own_rows = w1.T.astype(BF)
    own_cols = w1.astype(BF)

    def rs_out(s, k):
        return to_row(part.at[s, k], rec_e.at[s, k], rs_sem.at[s, k], re_sem.at[s, k], 1 + hi)

    def rs_cross(s, k):
        return to_row(part.at[s, k], rec_x.at[s, k], rs_sem.at[s, k], rx_sem.at[s, k], 3 - z)

    def rs_end(s, k):
        return to_row(part.at[s, k], rec_x.at[s, k], rs_sem.at[s, k], rx_sem.at[s, k], 3 * hi)

    def partial_sums(j, carry):
        mirrored = 3 - j + is_mid * (j // 2) * (2 * j - 5)
        s = row_of(mirrored)
        for k in range(nc):
            scores = mm(own_rows, fb[s, :, k * width:(k + 1) * width], 1, 0)
            part[s, k] = mm(own_cols, observed(s, k, scores), 1, 0)

        @pl.when((is_mid == 0) & (j < 3))
        def _():
            for k in range(nc):
                rs_out(s, k).start()

        return carry

    lax.fori_loop(0, 4, partial_sums, 0)

    for off in range(1, 4):
        peer = lax.rem(z + off, 4)
        to_row(wg.at[peer], wg.at[peer], ws_sem.at[peer], wr_sem.at[peer], peer).wait_recv()
        to_row(mown.at[peer], mrecv.at[peer], ms_sem.at[peer], mr_sem.at[peer], peer).wait_recv()
    for s in range(4):
        wrow[s] = wg[s].astype(F32).T.astype(BF)

    def solve_items(k, residual):
        start = v0b[z, :, pl.ds(pl.multiple_of(k * width, width), width)]

        def apply_a(i, p):
            pb = p.astype(BF)
            acc = ridge_i * p
            for s in range(0, 4, 2):
                scores = [mrecv[t, k] * mm(wrow[t], pb, 1, 0).astype(BF) for t in (s, s + 1)]
                both = jnp.concatenate([wg[s], wg[s + 1]], axis=1)
                acc = acc + mm(both, jnp.concatenate(scores, axis=0), 1, 0)
            return acc

        vout[z, k] = cg_steps(apply_a, start, residual - ridge_i * start)

    def ag(s, k, row, lane):
        return to_row(vout.at[s, k], vout.at[s, k], ag_sem.at[lane, s, k], agr_sem.at[s, k], row)

    def save(s, k):
        cols = pl.ds(pl.multiple_of(s * blk + k * width, width), width)
        return pltpu.make_async_copy(vout.at[s, k], v_out.at[:, cols], out_sem.at[s, k])

    def each(body):
        def step(k, carry):
            body(k)
            return carry

        lax.fori_loop(0, nc, step, 0)

    s0, s1, s2, s3 = (row_of(m) for m in range(4))

    @pl.when(is_mid == 0)
    def _():
        inner = 1 + hi

        def own(k):
            rs_end(s0, k).wait_recv()
            solve_items(k, part[s0, k] + rec_x[s0, k])
            ag(s0, k, inner, 0).start()
            save(s0, k).start()

        def take(s):
            def body(k):
                ag(s, k, inner, 0).wait_recv()
                save(s, k).start()

            return body

        def drain(k):
            for s in (s1, s2, s3):
                rs_out(s, k).wait_send()
            ag(s0, k, inner, 0).wait_send()

        each(own)
        for s in (s1, s2, s3):
            each(take(s))
        each(drain)

    @pl.when(is_mid == 1)
    def _():
        end, cross = 3 * hi, 3 - z

        def outer_to_cross(s):
            def body(k):
                rs_out(s, k).wait_recv()
                part[s, k] = part[s, k] + rec_e[s, k]
                rs_cross(s, k).start()

            return body

        def cross_to_end(k):
            rs_cross(s0, k).wait_recv()
            part[s0, k] = part[s0, k] + rec_x[s0, k]
            rs_end(s0, k).start()

        def own(k):
            rs_out(s1, k).wait_recv()
            rs_cross(s1, k).wait_recv()
            solve_items(k, part[s1, k] + (rec_e[s1, k] + rec_x[s1, k]))
            ag(s1, k, cross, 0).start()
            ag(s1, k, end, 1).start()
            save(s1, k).start()

        def relay(s, row):
            def body(k):
                ag(s, k, row, 0).wait_recv()
                ag(s, k, row, 0).start()
                save(s, k).start()

            return body

        def drain(k):
            for s in (s3, s2):
                rs_cross(s, k).wait_send()
            rs_end(s0, k).wait_send()
            ag(s1, k, cross, 0).wait_send()
            ag(s1, k, end, 1).wait_send()
            ag(s0, k, cross, 0).wait_send()
            ag(s2, k, end, 0).wait_send()
            ag(s3, k, end, 0).wait_send()

        each(outer_to_cross(s3))

        def both(k):
            outer_to_cross(s2)(k)
            cross_to_end(k)

        each(both)
        each(own)

        def relays(k):
            relay(s0, cross)(k)
            relay(s2, end)(k)

        each(relays)
        each(relay(s3, end))
        each(drain)

    for off in range(1, 4):
        peer = lax.rem(z + off, 4)
        to_row(wg.at[z], wg.at[z], ws_sem.at[peer], wr_sem.at[z], peer).wait_send()
        to_row(mown.at[peer], mrecv.at[z], ms_sem.at[peer], mr_sem.at[z], peer).wait_send()
        for rnd in range(CG_STEPS + 1):
            to_col(rnd, off).wait_send()
    for s in range(4):
        each(lambda k: save(s, k).wait())


def solution(mesh):
    row_size = mesh.shape["row"]
    col_size = mesh.shape["col"]
    assert row_size == 4 and col_size == 4
    grid_spec = P(("part", "row"), "col")
    user_spec = P(("part", "row"), None)
    item_spec = P(("part", "col"), None)

    def local_step(ratings, mask, user_blk, item_blk):
        users, items = ratings.shape
        rank = user_blk.shape[1]
        blk = items // row_size
        width = blk // CHUNKS
        ridge_u, ridge_i = RIDGE_WEIGHT * (items * col_size), RIDGE_WEIGHT * (users * row_size)
        vmem, any_space = pl.BlockSpec(memory_space=pltpu.VMEM), pl.BlockSpec(memory_space=pl.ANY)
        dma = pltpu.SemaphoreType.DMA
        sums = pltpu.VMEM((4, CHUNKS, rank, width), F32)
        user_new, item_new = pl.pallas_call(
            functools.partial(kernel, ridge_u, ridge_i),
            out_shape=(jax.ShapeDtypeStruct((rank, users), F32), jax.ShapeDtypeStruct((rank, items), F32)),
            in_specs=[any_space, any_space, vmem, any_space],
            out_specs=(vmem, any_space),
            scratch_shapes=[
                pltpu.VMEM((4, users, blk), jnp.int32),
                pltpu.VMEM((4, users, blk), F32),
                pltpu.VMEM((4, rank, blk), F32),
                pltpu.VMEM((4, rank, blk), BF),
                pltpu.VMEM((4, CHUNKS, users, width), BF),
                pltpu.VMEM((4, CHUNKS, users, width), BF),
                pltpu.VMEM((CG_STEPS + 1, 4, rank, users), F32),
                pltpu.VMEM((4, rank, users), BF),
                pltpu.VMEM((4, users, rank), BF),
                sums, sums, sums, sums,
                dma((3, 4)), dma((4,)), dma((4,)), dma((CG_STEPS + 1, 4)), dma((CG_STEPS + 1, 4)), dma((4,)), dma((4,)),
                dma((4, CHUNKS)), dma((4, CHUNKS)), dma((4, CHUNKS)), dma((2, 4, CHUNKS)), dma((4, CHUNKS)), dma((4, CHUNKS)),
            ],
            compiler_params=pltpu.CompilerParams(
                collective_id=0, has_side_effects=True, vmem_limit_bytes=56 * 2**20),
            name="als_sweep",
        )(ratings, mask, user_blk.T, item_blk.T)
        return user_new.T, item_new.T

    return jax.shard_map(local_step, mesh=mesh, in_specs=(grid_spec, grid_spec, user_spec, item_spec), out_specs=(user_spec, item_spec), check_vma=False)
```

time: 559 us -> 115 us (0.21)
  waiting for transfers between devices: 427 us -> 0 us
  Pallas kernels: 0 us -> 109 us
  blocking collectives: 54.4 us -> 0 us
  matrix products: 30.2 us -> 0 us
  other arithmetic: 29.1 us -> 0 us
  between operations: 14 us -> 0.64 us
    psum x5 -> x0, waiting for transfers between devices: 427 us -> none  [the longest x4 340 us: cg_block(): lax.psum(back_product(masked, fixed_bf, by_rows), axis_name)]
    pallas_call x0 -> x1, Pallas kernels: none -> 109 us  [local_step(): pl.pallas_call(functools.partial(kernel, ridge_u, ridge_i), out_shape=(ja...]
    psum x5 -> x0, blocking collectives: 54.4 us -> none  [the longest x4 41.5 us: cg_block(): lax.psum(back_product(masked, fixed_bf, by_rows), axis_name)]
    dot_general x10 -> x0, matrix products: 30.2 us -> none  [back_product(): lax.dot_general(block_bf, fixed_bf, (((contract,), (0,)), ((), ())), pref...]
    reduce_sum x14 -> x0, other arithmetic: 14.7 us -> none  [the longest x8 11 us: cg_block(): step_size = res_sq / jnp.sum(direction * gram_dir, axis=1, keepdims=True)]
    add x5 -> x0, other arithmetic: 8.23 us -> none  [the longest x1 4.62 us: cg_block(): estimate = estimate + step_size * direction]
  transfers between devices with their start and end apart: 5 -> 0, of which waited for: 5 -> 0; matrix products, arithmetic and copies ran while one was open for 0% -> 0% of each run, Pallas kernels for 0% -> 0%
where the time goes in v2:
time: 115 us; the launch traced here: 114 us
  Pallas kernels  109 us (95%)
  local copies, waits for them, and re-layouts  4.44 us (4%)
    pallas_call x1, Pallas kernels, local_step(): pl.pallas_call(functools.partial(kernel, ridge_u, ridge_i), out_shape=(ja...  109 us
    unnamed x2, local copies, waits for them, and re-layouts  4.44 us

profile of v2, /device:TPU:0, one launch (start us, length us, event | category | flops | bytes accessed | tf_op | source)
XLA Modules:
  0.0 114.3 jit_solution(10874372349142069214)
XLA Ops:
  0.6 109.2 %als_sweep.1 = (f32[64,128]{1,0:T(8,128)}, f32[64,8192]{1,0:T(8,128)}) custom-call(f32[128,8192]{1,0:T(8,128)} %r_hbm.1, s32[128,8192]{1,0:T(8,128)} %m_hbm.1, f32[64,128]{1,0:T(8,128)} %bitcast.6, f32[64,8192]{1,0:T(8,128)} %bitcast.4), custom_call_target="tpu_custom_call" | custom-call | tf_op jit(solution)/shard_map/als_sweep/pallas_call | solution.py:323
  109.9 1.4 %copy.8 = f32[128,64]{0,1:T(8,128)} copy(f32[128,64]{0,1:T(8,128)} %bitcast.7) | data formatting | bytes 65536
  111.3 3.1 %copy.9 = f32[8192,64]{0,1:T(8,128)} copy(f32[8192,64]{0,1:T(8,128)} %bitcast.5) | data formatting | bytes 4194304

commit v3 on v2

v3 whole, which is shorter than its diff:
```python
import functools

import jax
import jax.numpy as jnp
from jax import lax
from jax.experimental import pallas as pl
from jax.experimental.pallas import tpu as pltpu
from jax.sharding import PartitionSpec as P

CG_STEPS = 4
RIDGE_WEIGHT = 0.0005
CHUNKS = 8
CROSS_STEP = 1
OUT_AT, END_AT, OWN_AT, NEAR_AT, OUTER_AT, FAR_AT = (0, 3), (8, 2), (9, 2), (13, 2), (23, 1), (26, 1)
BF, F32 = jnp.bfloat16, jnp.float32
MESH = pl.DeviceIdType.MESH


def mm(a, b, contract_a, contract_b):
    return lax.dot_general(a, b, (((contract_a,), (contract_b,)), ((), ())), preferred_element_type=F32)


def col_sum(a, b):
    return jnp.sum(a * b, axis=0, keepdims=True)


def cg_steps(apply_a, start, residual):
    direction = residual
    estimate = start
    res_sq = col_sum(residual, residual)
    for cg_step in range(CG_STEPS):
        gram_dir = apply_a(direction)
        step_size = res_sq / col_sum(direction, gram_dir)
        estimate = estimate + step_size * direction
        if cg_step + 1 < CG_STEPS:
            residual = residual - step_size * gram_dir
            new_sq = col_sum(residual, residual)
            direction = residual + (new_sq / res_sq) * direction
            res_sq = new_sq
    return estimate


def kernel(
    ridge_u, ridge_i,
    r_hbm, m_hbm, w0_ref, v0_hbm,
    u_out, vout,
    mint, rbuf, v0b, fb, mown, mrecv, ar, wg, wrow, wcol, part, rec_e, rec_x,
    ld_sem, ms_sem, mr_sem, as_sem, arr_sem, ws_sem, wr_sem, rs_sem, re_sem, rx_sem, ag_sem, agr_sem,
):
    z = lax.axis_index("row")
    c = lax.axis_index("col")
    blk = mint.shape[2]
    nc, width = part.shape[1], part.shape[3]
    hi = z // 2
    is_mid = lax.rem(z + hi, 2)

    def row_of(mirrored):
        return mirrored + hi * (3 - 2 * mirrored)

    def to_row(src, dst, send, recv, row):
        return pltpu.make_async_remote_copy(
            src_ref=src, dst_ref=dst, send_sem=send, recv_sem=recv, device_id={"row": row}, device_id_type=MESH)

    def sent(buf, sem, n):
        src = buf if n is None or n == 1 else buf.at[:n]
        to_row(src, src, sem, sem, z).wait_send()

    cross, end = 3 - z, 3 * hi
    order = (3 - z, lax.rem(z + 2, 4), is_mid * end + (1 - is_mid) * (1 + hi), z)

    def load(hbm, buf, kind, s):
        return pltpu.make_async_copy(
            hbm.at[:, pl.ds(pl.multiple_of(s * blk, blk), blk)], buf.at[s], ld_sem.at[kind, s])

    barrier = pltpu.get_barrier_semaphore()
    load(m_hbm, mint, 0, order[0]).start()
    for off in (2, 3, 1):
        pl.semaphore_signal(barrier, inc=1, device_id={"row": lax.rem(z + off, 4)}, device_id_type=MESH)
    for off in range(1, 4):
        pl.semaphore_signal(barrier, inc=1, device_id={"col": lax.rem(c + off, 4)}, device_id_type=MESH)
    load(v0_hbm, v0b, 1, order[0]).start()
    load(r_hbm, rbuf, 2, order[0]).start()
    for s in order[1:]:
        load(m_hbm, mint, 0, s).start()
        load(v0_hbm, v0b, 1, s).start()
        load(r_hbm, rbuf, 2, s).start()

    def observed(s, k, scores):
        cols = pl.ds(pl.multiple_of(k * width, width), width)
        return jnp.where(mint[s, :, cols] > 0, rbuf[s, :, cols] - scores, 0.0).astype(BF)

    def send_mask(s):
        to_row(mown.at[s], mrecv.at[z], ms_sem, mr_sem.at[z], s).start()

    w0 = w0_ref[...]
    rows0 = w0.T.astype(BF)
    first = jnp.zeros((w0.shape[1], w0.shape[0]), F32)
    for j, s in enumerate(order):
        load(m_hbm, mint, 0, s).wait()
        for k in range(nc):
            m = mint[s, :, k * width:(k + 1) * width].astype(F32).astype(BF)
            mown[s, k] = m
            if j == 3:
                mrecv[z, k] = m
        if j == 0:
            pl.semaphore_wait(barrier, 6)
        if j == 2:
            send_mask(s)
        elif j < 2:
            @pl.when(is_mid == 0)
            def _():
                send_mask(s)
        load(v0_hbm, v0b, 1, s).wait()
        load(r_hbm, rbuf, 2, s).wait()
        for k in range(nc):
            cols = slice(k * width, (k + 1) * width)
            f = v0b[s, :, cols].astype(BF)
            fb[s, :, cols] = f
            first = first + mm(observed(s, k, mm(rows0, f, 1, 0)), f, 1, 1)

    def user_product(x):
        rows = x.T.astype(BF)
        acc = jnp.zeros((x.shape[1], x.shape[0]), F32)
        for s in range(4):
            for k in range(0, nc, 2):
                f = fb[s, :, k * width:(k + 2) * width]
                mask = jnp.concatenate([mown[s, k], mown[s, k + 1]], axis=1)
                acc = acc + mm(mask * mm(rows, f, 1, 0).astype(BF), f, 1, 1)
        return acc.T

    def to_col(rnd, off):
        peer = lax.rem(c + off, 4)
        return pltpu.make_async_remote_copy(
            src_ref=ar.at[rnd, c], dst_ref=ar.at[rnd, c], send_sem=as_sem, recv_sem=arr_sem.at[rnd, c],
            device_id={"col": peer}, device_id_type=MESH)

    def from_col(rnd, off):
        peer = lax.rem(c + off, 4)
        return pltpu.make_async_remote_copy(
            src_ref=ar.at[rnd, peer], dst_ref=ar.at[rnd, peer], send_sem=as_sem,
            recv_sem=arr_sem.at[rnd, peer], device_id={"col": peer}, device_id_type=MESH)

    def sum_cols(rnd, x):
        ar[rnd, c] = x
        for off in range(1, 4):
            to_col(rnd, off).start()
        for off in range(1, 4):
            from_col(rnd, off).wait_recv()
        return (ar[rnd, 0] + ar[rnd, 1]) + (ar[rnd, 2] + ar[rnd, 3])

    res = sum_cols(0, first.T) - ridge_u * w0

    def user_step(i, state):
        x, r, p, res_sq = state

        @pl.when((is_mid == 1) & (i == CROSS_STEP))
        def _():
            for s in order[:2]:
                send_mask(s)

        q = sum_cols(i + 1, user_product(p)) + ridge_u * p
        step_size = res_sq / col_sum(p, q)
        x = x + step_size * p
        r = r - step_size * q
        new_sq = col_sum(r, r)
        p = r + (new_sq / res_sq) * p
        return x, r, p, new_sq

    w1 = lax.fori_loop(0, CG_STEPS, user_step, (w0, res, res, col_sum(res, res)))[0]
    u_out[...] = w1

    wg[z] = w1.astype(BF)
    for off in range(1, 4):
        peer = lax.rem(z + off, 4)
        to_row(wg.at[z], wg.at[z], ws_sem, wr_sem.at[z], peer).start()

    own_rows = w1.T.astype(BF)
    own_cols = w1.astype(BF)

    def rs_out(s, k):
        return to_row(part.at[s, k], rec_e.at[s, k], rs_sem, re_sem.at[s, k], 1 + hi)

    def rs_cross(s, k):
        return to_row(part.at[s, k], rec_x.at[s, k], rs_sem, rx_sem.at[s, k], 3 - z)

    def rs_end(s, k):
        return to_row(part.at[s, k], rec_x.at[s, k], rs_sem, rx_sem.at[s, k], 3 * hi)

    def each(body, n=nc):
        def step(k, carry):
            body(k)
            return carry

        lax.fori_loop(0, n, step, 0)

    def outer_first(j):
        return row_of(3 - j)

    def partial_sums(k):
        for j in range(4):
            s = outer_first(j)
            f = fb[s, :, pl.ds(pl.multiple_of(k * width, width), width)]
            part[s, k] = mm(own_cols, observed(s, k, mm(own_rows, f, 1, 0)), 1, 0)

        @pl.when(is_mid == 0)
        def _():
            for j in range(3):
                rs_out(outer_first(j), k).start()

    each(partial_sums)

    def gather():
        for off in range(1, 4):
            peer = lax.rem(z + off, 4)
            to_row(wg.at[peer], wg.at[peer], ws_sem, wr_sem.at[peer], peer).wait_recv()
            to_row(mown.at[peer], mrecv.at[peer], ms_sem, mr_sem.at[peer], peer).wait_recv()
        users = own_rows.shape[0]
        for s in range(4):
            wrow[s * users:(s + 1) * users] = wg[s].astype(F32).T.astype(BF)
            wcol[:, s * users:(s + 1) * users] = wg[s]

    def cols_of(s, k):
        return pl.ds(pl.multiple_of(s * blk + k * width, width), width)

    def solve_items(k, residual):
        start = v0b[z, :, pl.ds(pl.multiple_of(k * width, width), width)]

        def apply_a(p):
            masked = jnp.concatenate([mrecv[t, k] for t in range(4)], axis=0)
            masked = masked * mm(wrow[...], p.astype(BF), 1, 0).astype(BF)
            return mm(wcol[...], masked, 1, 0) + ridge_i * p

        vout[:, cols_of(z, k)] = cg_steps(apply_a, start, residual - ridge_i * start)

    def ag(s, k, row):
        chunk = vout.at[:, cols_of(s, k)]
        return to_row(chunk, chunk, ag_sem, agr_sem.at[s, k], row)

    s0, s1, s2, s3 = (row_of(m) for m in range(4))

    @pl.when(is_mid == 0)
    def _():
        inner = 1 + hi

        def own(k):
            rs_end(s0, k).wait_recv()
            solve_items(k, part[s0, k] + rec_x[s0, k])
            ag(s0, k, inner).start()

        def take(s):
            def body(k):
                ag(s, k, inner).wait_recv()

            return body

        gather()
        each(own)
        for s in (s1, s2, s3):
            each(take(s))
        sent(part, rs_sem, 3)
        sent(vout.at[:, :blk], ag_sem, 1)

    @pl.when(is_mid == 1)
    def _():
        def outer_to_cross(s):
            def body(k):
                rs_out(s, k).wait_recv()
                part[s, k] = part[s, k] + rec_e[s, k]
                rs_cross(s, k).start()

            return body

        def cross_to_end(k):
            rs_cross(s0, k).wait_recv()
            part[s0, k] = part[s0, k] + rec_x[s0, k]
            rs_end(s0, k).start()

        def own(k):
            rs_out(s1, k).wait_recv()
            rs_cross(s1, k).wait_recv()
            solve_items(k, part[s1, k] + (rec_e[s1, k] + rec_x[s1, k]))
            ag(s1, k, cross).start()
            ag(s1, k, end).start()

        def relay(s, row):
            def body(k):
                ag(s, k, row).wait_recv()
                ag(s, k, row).start()

            return body

        def out(k):
            outer_to_cross(s3)(k)
            outer_to_cross(s2)(k)

        work = (
            (OUT_AT, out), (END_AT, cross_to_end), (OWN_AT, own),
            (NEAR_AT, relay(s2, end)), (OUTER_AT, relay(s0, cross)), (FAR_AT, relay(s3, end)),
        )

        def step(t):
            @pl.when(t == OWN_AT[0])
            def _():
                gather()

            for (at, every), body in work:
                k = (t - at + every * nc) // every - nc

                @pl.when((k >= 0) & (k < nc) & (at + k * every == t))
                def _():
                    body(k)

        each(step, max(at + every * (nc - 1) for (at, every), _ in work) + 1)
        sent(part, rs_sem, 3)
        for _ in range(5):
            sent(vout.at[:, :blk], ag_sem, 1)

    sent(wg, ws_sem, 3)
    sent(mown, ms_sem, 3)
    sent(ar.at[:, :3], as_sem, None)


def finish_kernel(u_in, v_in, u_out, v_out, sem):
    copies = [pltpu.make_async_copy(v_in, v_out, sem.at[0]), pltpu.make_async_copy(u_in, u_out, sem.at[1])]
    for copy in copies:
        copy.start()
    for copy in copies:
        copy.wait()


def solution(mesh):
    row_size = mesh.shape["row"]
    col_size = mesh.shape["col"]
    assert row_size == 4 and col_size == 4
    grid_spec = P(("part", "row"), "col")
    user_spec = P(("part", "row"), None)
    item_spec = P(("part", "col"), None)

    def local_step(ratings, mask, user_blk, item_blk):
        users, items = ratings.shape
        rank = user_blk.shape[1]
        blk = items // row_size
        width = blk // CHUNKS
        ridge_u, ridge_i = RIDGE_WEIGHT * (items * col_size), RIDGE_WEIGHT * (users * row_size)
        vmem, any_space = pl.BlockSpec(memory_space=pltpu.VMEM), pl.BlockSpec(memory_space=pl.ANY)
        dma = pltpu.SemaphoreType.DMA
        sums = pltpu.VMEM((4, CHUNKS, rank, width), F32)
        user_new, item_new = pl.pallas_call(
            functools.partial(kernel, ridge_u, ridge_i),
            out_shape=(pltpu.VMEM((rank, users), F32), pltpu.VMEM((rank, items), F32)),
            in_specs=[any_space, any_space, vmem, any_space],
            out_specs=(vmem, vmem),
            scratch_shapes=[
                pltpu.VMEM((4, users, blk), jnp.int32),
                pltpu.VMEM((4, users, blk), F32),
                pltpu.VMEM((4, rank, blk), F32),
                pltpu.VMEM((4, rank, blk), BF),
                pltpu.VMEM((4, CHUNKS, users, width), BF),
                pltpu.VMEM((4, CHUNKS, users, width), BF),
                pltpu.VMEM((CG_STEPS + 1, 4, rank, users), F32),
                pltpu.VMEM((4, rank, users), BF),
                pltpu.VMEM((4 * users, rank), BF),
                pltpu.VMEM((rank, 4 * users), BF),
                sums, sums, sums,
                dma((3, 4)), dma, dma((4,)), dma, dma((CG_STEPS + 1, 4)), dma, dma((4,)),
                dma, dma((4, CHUNKS)), dma((4, CHUNKS)), dma, dma((4, CHUNKS)),
            ],
            compiler_params=pltpu.CompilerParams(
                collective_id=0, has_side_effects=True, vmem_limit_bytes=56 * 2**20),
            name="als_sweep",
        )(ratings, mask, user_blk.T, item_blk.T)
        user_new, item_new = pl.pallas_call(
            finish_kernel,
            out_shape=(jax.ShapeDtypeStruct((rank, users), F32), jax.ShapeDtypeStruct((rank, items), F32)),
            in_specs=[vmem, vmem],
            out_specs=(any_space, any_space),
            scratch_shapes=[dma((2,))],
            name="write_out",
        )(*(pltpu.with_memory_space_constraint(x, pltpu.VMEM) for x in (user_new, item_new)))
        return user_new.T, item_new.T

    return jax.shard_map(local_step, mesh=mesh, in_specs=(grid_spec, grid_spec, user_spec, item_spec), out_specs=(user_spec, item_spec), check_vma=False)
```

time: 115 us -> 109 us (0.948)
  local copies, waits for them, and re-layouts: 4.44 us -> 0 us
    unnamed x2 -> x0, local copies, waits for them, and re-layouts: 4.44 us -> none
    pallas_call x1 -> x2, Pallas kernels: 109 us -> 108 us  [the longest x1 107 us: local_step(): pl.pallas_call(functools.partial(kernel, ridge_u, ridge_i), out_shape=(pl...]
where the time goes in v3:
time: 109 us
  Pallas kernels  108 us (99%)
    pallas_call x1, Pallas kernels, local_step(): pl.pallas_call(functools.partial(kernel, ridge_u, ridge_i), out_shape=(pl...  107 us

profile of v3, /device:TPU:0, one launch (start us, length us, event | category | flops | bytes accessed | tf_op | source)
XLA Modules:
  0.0 109.0 jit_solution(16887795691031988410)
XLA Ops:
  0.6 107.1 %als_sweep.1 = (f32[64,128]{1,0:T(8,128)S(1)}, f32[64,8192]{1,0:T(8,128)S(1)}) custom-call(f32[128,8192]{1,0:T(8,128)} %r_hbm.1, s32[128,8192]{1,0:T(8,128)} %m_hbm.1, f32[64,128]{1,0:T(8,128)} %bitcast.5, f32[64,8192]{1,0:T(8,128)} %bitcast.4), custom_call_target="tpu_custom_call" | custom-call | tf_op jit(solution)/shard_map/als_sweep/pallas_call | solution.py:348
  107.7 1.3 %write_out.1 = (f32[64,128]{1,0:T(8,128)}, f32[64,8192]{1,0:T(8,128)}) custom-call(f32[64,128]{1,0:T(8,128)S(1)} %get-tuple-element.6.u_in, f32[64,8192]{1,0:T(8,128)S(1)} %get-tuple-element.7.v_in), custom_call_target="tpu_custom_call" | custom-call | tf_op jit(solution)/shard_map/write_out/pallas_call | solution.py:372

commit v4 on v3

--- a/solution.py
+++ b/solution.py
@@ -10,8 +10,18 @@
 CG_STEPS = 4
 RIDGE_WEIGHT = 0.0005
 CHUNKS = 8
-CROSS_STEP = 1
-OUT_AT, END_AT, OWN_AT, NEAR_AT, OUTER_AT, FAR_AT = (0, 3), (8, 2), (9, 2), (13, 2), (23, 1), (26, 1)
+FAR_SUM, NEAR_SUM, END_SUM, NEAR_RES, END_RES, FAR_RES = range(6)
+RELAYS = (
+    ((FAR_SUM, 0), (NEAR_SUM, 0), (FAR_SUM, 1), (NEAR_SUM, 1), (FAR_SUM, 2), (END_SUM, 0), (NEAR_SUM, 2)),
+    ((END_SUM, 1), (FAR_SUM, 3)),
+    ((NEAR_SUM, 3), (END_SUM, 2)),
+    ((FAR_SUM, 4), (NEAR_RES, 0), (NEAR_SUM, 4), (END_SUM, 3), (NEAR_RES, 1), (FAR_SUM, 5)),
+    ((NEAR_SUM, 5), (NEAR_RES, 2), (END_SUM, 4), (FAR_SUM, 6)),
+    ((NEAR_SUM, 6), (END_SUM, 5), (NEAR_RES, 3), (FAR_SUM, 7)),
+    ((NEAR_SUM, 7), (END_SUM, 6), (NEAR_RES, 4), (END_RES, 0)),
+    ((END_SUM, 7), (END_RES, 1), (END_RES, 2), (NEAR_RES, 5), (END_RES, 3)),
+    ((END_RES, 4), (FAR_RES, 0), (END_RES, 5), (NEAR_RES, 6), (END_RES, 6), (FAR_RES, 1), (FAR_RES, 2), (FAR_RES, 3), (END_RES, 7), (NEAR_RES, 7), (FAR_RES, 4), (FAR_RES, 5), (FAR_RES, 6), (FAR_RES, 7)),
+)
 BF, F32 = jnp.bfloat16, jnp.float32
 MESH = pl.DeviceIdType.MESH
 
@@ -45,7 +55,7 @@
     r_hbm, m_hbm, w0_ref, v0_hbm,
     u_out, vout,
     mint, rbuf, v0b, fb, mown, mrecv, ar, wg, wrow, wcol, part, rec_e, rec_x,
-    ld_sem, ms_sem, mr_sem, as_sem, arr_sem, ws_sem, wr_sem, rs_sem, re_sem, rx_sem, ag_sem, agr_sem,
+    ld_sem, ms_sem, mr_sem, as_sem, arr_sem, ws_sem, wr_sem, rs_sem, chunk_sem, across_sem, ag_sem, near_sem, far_sem,
 ):
     z = lax.axis_index("row")
     c = lax.axis_index("col")
@@ -62,11 +72,11 @@
             src_ref=src, dst_ref=dst, send_sem=send, recv_sem=recv, device_id={"row": row}, device_id_type=MESH)
 
     def sent(buf, sem, n):
-        src = buf if n is None or n == 1 else buf.at[:n]
+        src = buf if n is None else buf.at[:n]
         to_row(src, src, sem, sem, z).wait_send()
 
     cross, end = 3 - z, 3 * hi
-    order = (3 - z, lax.rem(z + 2, 4), is_mid * end + (1 - is_mid) * (1 + hi), z)
+    order = (2 - hi, 3 - 3 * hi, is_mid * end + (1 - is_mid) * (1 + hi), z)
 
     def load(hbm, buf, kind, s):
         return pltpu.make_async_copy(
@@ -74,8 +84,19 @@
 
     barrier = pltpu.get_barrier_semaphore()
     load(m_hbm, mint, 0, order[0]).start()
-    for off in (2, 3, 1):
-        pl.semaphore_signal(barrier, inc=1, device_id={"row": lax.rem(z + off, 4)}, device_id_type=MESH)
+
+    def tell(sem, row):
+        pl.semaphore_signal(sem, inc=1, device_id={"row": row}, device_id_type=MESH)
+
+    @pl.when(is_mid == 1)
+    def _():
+        tell(barrier, cross)
+        tell(barrier, end)
+
+    @pl.when(is_mid == 0)
+    def _():
+        tell(barrier, 1 + hi)
+
     for off in range(1, 4):
         pl.semaphore_signal(barrier, inc=1, device_id={"col": lax.rem(c + off, 4)}, device_id_type=MESH)
     load(v0_hbm, v0b, 1, order[0]).start()
@@ -103,13 +124,26 @@
             if j == 3:
                 mrecv[z, k] = m
         if j == 0:
-            pl.semaphore_wait(barrier, 6)
-        if j == 2:
-            send_mask(s)
-        elif j < 2:
+            pl.semaphore_wait(barrier, 4 + is_mid)
+
+            @pl.when(is_mid == 1)
+            def _():
+                tell(far_sem, cross)
+                tell(near_sem, end)
+
             @pl.when(is_mid == 0)
             def _():
-                send_mask(s)
+                pl.semaphore_wait(near_sem, 1)
+
+        if j == 1:
+            pl.semaphore_wait(far_sem, 1)
+
+            @pl.when(is_mid == 1)
+            def _():
+                tell(far_sem, end)
+
+        if j < 3:
+            send_mask(s)
         load(v0_hbm, v0b, 1, s).wait()
         load(r_hbm, rbuf, 2, s).wait()
         for k in range(nc):
@@ -131,14 +165,14 @@
     def to_col(rnd, off):
         peer = lax.rem(c + off, 4)
         return pltpu.make_async_remote_copy(
-            src_ref=ar.at[rnd, c], dst_ref=ar.at[rnd, c], send_sem=as_sem, recv_sem=arr_sem.at[rnd, c],
+            src_ref=ar.at[rnd, c], dst_ref=ar.at[rnd, c], send_sem=as_sem, recv_sem=arr_sem.at[lax.rem(rnd, 2), c],
             device_id={"col": peer}, device_id_type=MESH)
 
     def from_col(rnd, off):
         peer = lax.rem(c + off, 4)
         return pltpu.make_async_remote_copy(
             src_ref=ar.at[rnd, peer], dst_ref=ar.at[rnd, peer], send_sem=as_sem,
-            recv_sem=arr_sem.at[rnd, peer], device_id={"col": peer}, device_id_type=MESH)
+            recv_sem=arr_sem.at[lax.rem(rnd, 2), peer], device_id={"col": peer}, device_id_type=MESH)
 
     def sum_cols(rnd, x):
         ar[rnd, c] = x
@@ -153,11 +187,6 @@
     def user_step(i, state):
         x, r, p, res_sq = state
 
-        @pl.when((is_mid == 1) & (i == CROSS_STEP))
-        def _():
-            for s in order[:2]:
-                send_mask(s)
-
         q = sum_cols(i + 1, user_product(p)) + ridge_u * p
         step_size = res_sq / col_sum(p, q)
         x = x + step_size * p
@@ -169,22 +198,31 @@
     w1 = lax.fori_loop(0, CG_STEPS, user_step, (w0, res, res, col_sum(res, res)))[0]
     u_out[...] = w1
 
+    def give(src_row, row):
+        return to_row(wg.at[src_row], wg.at[src_row], ws_sem, wr_sem.at[src_row], row)
+
     wg[z] = w1.astype(BF)
-    for off in range(1, 4):
-        peer = lax.rem(z + off, 4)
-        to_row(wg.at[z], wg.at[z], ws_sem, wr_sem.at[z], peer).start()
+
+    @pl.when(is_mid == 0)
+    def _():
+        give(z, 1 + hi).start()
+
+    @pl.when(is_mid == 1)
+    def _():
+        give(z, cross).start()
+        give(z, end).start()
 
     own_rows = w1.T.astype(BF)
     own_cols = w1.astype(BF)
 
     def rs_out(s, k):
-        return to_row(part.at[s, k], rec_e.at[s, k], rs_sem, re_sem.at[s, k], 1 + hi)
-
-    def rs_cross(s, k):
-        return to_row(part.at[s, k], rec_x.at[s, k], rs_sem, rx_sem.at[s, k], 3 - z)
+        return to_row(part.at[s, k], rec_e.at[s, k], rs_sem, chunk_sem.at[s, k], 1 + hi)
+
+    def rs_cross(s, k, sem):
+        return to_row(part.at[s, k], rec_x.at[s, k], rs_sem, sem, cross)
 
     def rs_end(s, k):
-        return to_row(part.at[s, k], rec_x.at[s, k], rs_sem, rx_sem.at[s, k], 3 * hi)
+        return to_row(part.at[s, k], rec_x.at[s, k], rs_sem, chunk_sem.at[s, k], end)
 
     def each(body, n=nc):
         def step(k, carry):
@@ -212,7 +250,14 @@
     def gather():
         for off in range(1, 4):
             peer = lax.rem(z + off, 4)
-            to_row(wg.at[peer], wg.at[peer], ws_sem, wr_sem.at[peer], peer).wait_recv()
+            @pl.when((is_mid == 0) | (peer != end))
+            def _():
+                give(peer, end).wait_recv()
+
+            @pl.when((is_mid == 1) & (peer != end))
+            def _():
+                give(peer, end).start()
+
             to_row(mown.at[peer], mrecv.at[peer], ms_sem, mr_sem.at[peer], peer).wait_recv()
         users = own_rows.shape[0]
         for s in range(4):
@@ -234,7 +279,7 @@
 
     def ag(s, k, row):
         chunk = vout.at[:, cols_of(s, k)]
-        return to_row(chunk, chunk, ag_sem, agr_sem.at[s, k], row)
+        return to_row(chunk, chunk, ag_sem, chunk_sem.at[s, k], row)
 
     s0, s1, s2, s3 = (row_of(m) for m in range(4))
 
@@ -257,27 +302,28 @@
         each(own)
         for s in (s1, s2, s3):
             each(take(s))
+        sent(wg, ws_sem, 1)
         sent(part, rs_sem, 3)
-        sent(vout.at[:, :blk], ag_sem, 1)
+        sent(vout.at[:, :blk], ag_sem, None)
 
     @pl.when(is_mid == 1)
     def _():
-        def outer_to_cross(s):
+        def outer_to_cross(s, sem):
             def body(k):
                 rs_out(s, k).wait_recv()
                 part[s, k] = part[s, k] + rec_e[s, k]
-                rs_cross(s, k).start()
+                rs_cross(s, k, sem(k)).start()
 
             return body
 
         def cross_to_end(k):
-            rs_cross(s0, k).wait_recv()
+            rs_cross(s0, k, chunk_sem.at[s0, k]).wait_recv()
             part[s0, k] = part[s0, k] + rec_x[s0, k]
             rs_end(s0, k).start()
 
         def own(k):
             rs_out(s1, k).wait_recv()
-            rs_cross(s1, k).wait_recv()
+            rs_cross(s1, k, across_sem.at[k]).wait_recv()
             solve_items(k, part[s1, k] + (rec_e[s1, k] + rec_x[s1, k]))
             ag(s1, k, cross).start()
             ag(s1, k, end).start()
@@ -289,33 +335,30 @@
 
             return body
 
-        def out(k):
-            outer_to_cross(s3)(k)
-            outer_to_cross(s2)(k)
-
-        work = (
-            (OUT_AT, out), (END_AT, cross_to_end), (OWN_AT, own),
-            (NEAR_AT, relay(s2, end)), (OUTER_AT, relay(s0, cross)), (FAR_AT, relay(s3, end)),
+        relays = (
+            outer_to_cross(s3, lambda k: chunk_sem.at[s3, k]), outer_to_cross(s2, lambda k: across_sem.at[k]), cross_to_end, relay(s2, end), relay(s0, cross), relay(s3, end),
         )
-
-        def step(t):
-            @pl.when(t == OWN_AT[0])
-            def _():
-                gather()
-
-            for (at, every), body in work:
-                k = (t - at + every * nc) // every - nc
-
-                @pl.when((k >= 0) & (k < nc) & (at + k * every == t))
+        give(end, cross).wait_recv()
+        give(end, cross).start()
+        for kind, k in RELAYS[0]:
+            relays[kind](k)
+        gather()
+
+        def step(j):
+            own(j)
+            for i in range(nc):
+                @pl.when(j == i)
                 def _():
-                    body(k)
-
-        each(step, max(at + every * (nc - 1) for (at, every), _ in work) + 1)
+                    for kind, k in RELAYS[i + 1]:
+                        relays[kind](k)
+
+        each(step)
+        sent(wg, ws_sem, 4)
+        sent(wg, ws_sem, 1)
         sent(part, rs_sem, 3)
         for _ in range(5):
-            sent(vout.at[:, :blk], ag_sem, 1)
-
-    sent(wg, ws_sem, 3)
+            sent(vout.at[:, :blk], ag_sem, None)
+
     sent(mown, ms_sem, 3)
     sent(ar.at[:, :3], as_sem, None)
 
@@ -362,8 +405,9 @@
                 pltpu.VMEM((4 * users, rank), BF),
                 pltpu.VMEM((rank, 4 * users), BF),
                 sums, sums, sums,
-                dma((3, 4)), dma, dma((4,)), dma, dma((CG_STEPS + 1, 4)), dma, dma((4,)),
-                dma, dma((4, CHUNKS)), dma((4, CHUNKS)), dma, dma((4, CHUNKS)),
+                dma((3, 4)), dma, dma((4,)), dma, dma((2, 4)), dma, dma((4,)),
+                dma, dma((4, CHUNKS)), dma((CHUNKS,)), dma,
+                pltpu.SemaphoreType.REGULAR, pltpu.SemaphoreType.REGULAR,
             ],
             compiler_params=pltpu.CompilerParams(
                 collective_id=0, has_side_effects=True, vmem_limit_bytes=56 * 2**20),

time: 109 us -> 105 us (0.963)
  Pallas kernels: 108 us -> 104 us
    pallas_call x1, Pallas kernels: 107 us -> 103 us  [local_step(): pl.pallas_call(functools.partial(kernel, ridge_u, ridge_i), out_shape=(pl...]
where the time goes in v4:
time: 105 us
  Pallas kernels  104 us (99%)
    pallas_call x1, Pallas kernels, local_step(): pl.pallas_call(functools.partial(kernel, ridge_u, ridge_i), out_shape=(pl...  103 us

profile of v4, /device:TPU:0, one launch (start us, length us, event | category | flops | bytes accessed | tf_op | source)
XLA Modules:
  0.0 104.8 jit_solution(16682712849162671613)
XLA Ops:
  0.6 102.9 %als_sweep.1 = (f32[64,128]{1,0:T(8,128)S(1)}, f32[64,8192]{1,0:T(8,128)S(1)}) custom-call(f32[128,8192]{1,0:T(8,128)} %r_hbm.1, s32[128,8192]{1,0:T(8,128)} %m_hbm.1, f32[64,128]{1,0:T(8,128)} %bitcast.5, f32[64,8192]{1,0:T(8,128)} %bitcast.4), custom_call_target="tpu_custom_call" | custom-call | tf_op jit(solution)/shard_map/als_sweep/pallas_call | solution.py:391
  103.5 1.3 %write_out.1 = (f32[64,128]{1,0:T(8,128)}, f32[64,8192]{1,0:T(8,128)}) custom-call(f32[64,128]{1,0:T(8,128)S(1)} %get-tuple-element.6.u_in, f32[64,8192]{1,0:T(8,128)S(1)} %get-tuple-element.7.v_in), custom_call_target="tpu_custom_call" | custom-call | tf_op jit(solution)/shard_map/write_out/pallas_call | solution.py:416

commit v5 on v4

--- a/solution.py
+++ b/solution.py
@@ -22,6 +22,7 @@
     ((END_SUM, 7), (END_RES, 1), (END_RES, 2), (NEAR_RES, 5), (END_RES, 3)),
     ((END_RES, 4), (FAR_RES, 0), (END_RES, 5), (NEAR_RES, 6), (END_RES, 6), (FAR_RES, 1), (FAR_RES, 2), (FAR_RES, 3), (END_RES, 7), (NEAR_RES, 7), (FAR_RES, 4), (FAR_RES, 5), (FAR_RES, 6), (FAR_RES, 7)),
 )
+HOLD = 3
 BF, F32 = jnp.bfloat16, jnp.float32
 MESH = pl.DeviceIdType.MESH
 
@@ -55,7 +56,7 @@
     r_hbm, m_hbm, w0_ref, v0_hbm,
     u_out, vout,
     mint, rbuf, v0b, fb, mown, mrecv, ar, wg, wrow, wcol, part, rec_e, rec_x,
-    ld_sem, ms_sem, mr_sem, as_sem, arr_sem, ws_sem, wr_sem, rs_sem, chunk_sem, across_sem, ag_sem, near_sem, far_sem,
+    ld_sem, v_sem, r_sem, ms_sem, mr_sem, as_sem, arr_sem, ws_sem, wr_sem, rs_sem, chunk_sem, across_sem, ag_sem, near_sem, far_sem,
 ):
     z = lax.axis_index("row")
     c = lax.axis_index("col")
@@ -78,12 +79,11 @@
     cross, end = 3 - z, 3 * hi
     order = (2 - hi, 3 - 3 * hi, is_mid * end + (1 - is_mid) * (1 + hi), z)
 
-    def load(hbm, buf, kind, s):
-        return pltpu.make_async_copy(
-            hbm.at[:, pl.ds(pl.multiple_of(s * blk, blk), blk)], buf.at[s], ld_sem.at[kind, s])
+    def load(hbm, buf, s, sem):
+        return pltpu.make_async_copy(hbm.at[:, pl.ds(pl.multiple_of(s * blk, blk), blk)], buf.at[s], sem)
 
     barrier = pltpu.get_barrier_semaphore()
-    load(m_hbm, mint, 0, order[0]).start()
+    load(m_hbm, mint, order[0], ld_sem.at[0]).start()
 
     def tell(sem, row):
         pl.semaphore_signal(sem, inc=1, device_id={"row": row}, device_id_type=MESH)
@@ -99,13 +99,6 @@
 
     for off in range(1, 4):
         pl.semaphore_signal(barrier, inc=1, device_id={"col": lax.rem(c + off, 4)}, device_id_type=MESH)
-    load(v0_hbm, v0b, 1, order[0]).start()
-    load(r_hbm, rbuf, 2, order[0]).start()
-    for s in order[1:]:
-        load(m_hbm, mint, 0, s).start()
-        load(v0_hbm, v0b, 1, s).start()
-        load(r_hbm, rbuf, 2, s).start()
-
     def observed(s, k, scores):
         cols = pl.ds(pl.multiple_of(k * width, width), width)
         return jnp.where(mint[s, :, cols] > 0, rbuf[s, :, cols] - scores, 0.0).astype(BF)
@@ -117,7 +110,7 @@
     rows0 = w0.T.astype(BF)
     first = jnp.zeros((w0.shape[1], w0.shape[0]), F32)
     for j, s in enumerate(order):
-        load(m_hbm, mint, 0, s).wait()
+        load(m_hbm, mint, s, ld_sem.at[j]).wait()
         for k in range(nc):
             m = mint[s, :, k * width:(k + 1) * width].astype(F32).astype(BF)
             mown[s, k] = m
@@ -144,8 +137,14 @@
 
         if j < 3:
             send_mask(s)
-        load(v0_hbm, v0b, 1, s).wait()
-        load(r_hbm, rbuf, 2, s).wait()
+        if j == 0:
+            for i, other in enumerate(order):
+                if i:
+                    load(m_hbm, mint, other, ld_sem.at[i]).start()
+                load(v0_hbm, v0b, other, v_sem).start()
+                load(r_hbm, rbuf, other, r_sem).start()
+            pltpu.make_async_copy(v0b, v0b, v_sem).wait()
+            pltpu.make_async_copy(rbuf, rbuf, r_sem).wait()
         for k in range(nc):
             cols = slice(k * width, (k + 1) * width)
             f = v0b[s, :, cols].astype(BF)
@@ -271,9 +270,13 @@
         start = v0b[z, :, pl.ds(pl.multiple_of(k * width, width), width)]
 
         def apply_a(p):
-            masked = jnp.concatenate([mrecv[t, k] for t in range(4)], axis=0)
-            masked = masked * mm(wrow[...], p.astype(BF), 1, 0).astype(BF)
-            return mm(wcol[...], masked, 1, 0) + ridge_i * p
+            pb = p.astype(BF)
+            users = wrow.shape[0] // 2
+            halves = []
+            for i in range(2):
+                mask = jnp.concatenate([mrecv[2 * i, k], mrecv[2 * i + 1, k]], axis=0)
+                halves.append(mask * mm(wrow[i * users:(i + 1) * users], pb, 1, 0).astype(BF))
+            return mm(wcol[...], jnp.concatenate(halves, axis=0), 1, 0) + ridge_i * p
 
         vout[:, cols_of(z, k)] = cg_steps(apply_a, start, residual - ridge_i * start)
 
@@ -335,8 +338,26 @@
 
             return body
 
+        def held_relay(s, row):
+            def body(k):
+                ag(s, k, row).wait_recv()
+
+                @pl.when(lax.rem(c, 2) == 0)
+                def _():
+                    ag(s, k, row).start()
+
+                @pl.when(lax.rem(c, 2) == 1)
+                def _():
+                    if k >= HOLD:
+                        ag(s, k - HOLD, row).start()
+                    if k == nc - 1:
+                        for i in range(nc - HOLD, nc):
+                            ag(s, i, row).start()
+
+            return body
+
         relays = (
-            outer_to_cross(s3, lambda k: chunk_sem.at[s3, k]), outer_to_cross(s2, lambda k: across_sem.at[k]), cross_to_end, relay(s2, end), relay(s0, cross), relay(s3, end),
+            outer_to_cross(s3, lambda k: chunk_sem.at[s3, k]), outer_to_cross(s2, lambda k: across_sem.at[k]), cross_to_end, relay(s2, end), held_relay(s0, cross), relay(s3, end),
         )
         give(end, cross).wait_recv()
         give(end, cross).start()
@@ -405,7 +426,7 @@
                 pltpu.VMEM((4 * users, rank), BF),
                 pltpu.VMEM((rank, 4 * users), BF),
                 sums, sums, sums,
-                dma((3, 4)), dma, dma((4,)), dma, dma((2, 4)), dma, dma((4,)),
+                dma((4,)), dma, dma, dma, dma((4,)), dma, dma((2, 4)), dma, dma((4,)),
                 dma, dma((4, CHUNKS)), dma((CHUNKS,)), dma,
                 pltpu.SemaphoreType.REGULAR, pltpu.SemaphoreType.REGULAR,
             ],

time: 105 us -> 104 us (level)
  no operation moved by 1% of the time
where the time goes in v5:
time: 104 us
  Pallas kernels  103 us (99%)
    pallas_call x1, Pallas kernels, local_step(): pl.pallas_call(functools.partial(kernel, ridge_u, ridge_i), out_shape=(pl...  102 us

profile of v5, /device:TPU:0, one launch (start us, length us, event | category | flops | bytes accessed | tf_op | source)
XLA Modules:
  0.0 104.1 jit_solution(2308576646536477274)
XLA Ops:
  0.6 102.2 %als_sweep.1 = (f32[64,128]{1,0:T(8,128)S(1)}, f32[64,8192]{1,0:T(8,128)S(1)}) custom-call(f32[128,8192]{1,0:T(8,128)} %r_hbm.1, s32[128,8192]{1,0:T(8,128)} %m_hbm.1, f32[64,128]{1,0:T(8,128)} %bitcast.5, f32[64,8192]{1,0:T(8,128)} %bitcast.4), custom_call_target="tpu_custom_call" | custom-call | tf_op jit(solution)/shard_map/als_sweep/pallas_call | solution.py:412
  102.8 1.3 %write_out.1 = (f32[64,128]{1,0:T(8,128)}, f32[64,8192]{1,0:T(8,128)}) custom-call(f32[64,128]{1,0:T(8,128)S(1)} %get-tuple-element.6.u_in, f32[64,8192]{1,0:T(8,128)S(1)} %get-tuple-element.7.v_in), custom_call_target="tpu_custom_call" | custom-call | tf_op jit(solution)/shard_map/write_out/pallas_call | solution.py:437

commit v6 on v5

--- a/solution.py
+++ b/solution.py
@@ -53,10 +53,10 @@
 
 def kernel(
     ridge_u, ridge_i,
-    r_hbm, m_hbm, w0_ref, v0_hbm,
+    r_hbm, m_hbm, w0_hbm, v0_hbm,
     u_out, vout,
-    mint, rbuf, v0b, fb, mown, mrecv, ar, wg, wrow, wcol, part, rec_e, rec_x,
-    ld_sem, v_sem, r_sem, ms_sem, mr_sem, as_sem, arr_sem, ws_sem, wr_sem, rs_sem, chunk_sem, across_sem, ag_sem, near_sem, far_sem,
+    w0_ref, mint, rbuf, v0b, fb, mown, mrecv, ar, wg, wrow, wcol, part, rec_e, rec_x,
+    ld_sem, w_sem, v_sem, r_sem, ms_sem, mr_sem, as_sem, arr_sem, ws_sem, wr_sem, rs_sem, chunk_sem, across_sem, ag_sem, near_sem, far_sem,
 ):
     z = lax.axis_index("row")
     c = lax.axis_index("col")
@@ -106,9 +106,7 @@
     def send_mask(s):
         to_row(mown.at[s], mrecv.at[z], ms_sem, mr_sem.at[z], s).start()
 
-    w0 = w0_ref[...]
-    rows0 = w0.T.astype(BF)
-    first = jnp.zeros((w0.shape[1], w0.shape[0]), F32)
+    first = jnp.zeros(w0_ref.shape[::-1], F32)
     for j, s in enumerate(order):
         load(m_hbm, mint, s, ld_sem.at[j]).wait()
         for k in range(nc):
@@ -138,11 +136,15 @@
         if j < 3:
             send_mask(s)
         if j == 0:
+            pltpu.make_async_copy(w0_hbm, w0_ref, w_sem).start()
             for i, other in enumerate(order):
                 if i:
                     load(m_hbm, mint, other, ld_sem.at[i]).start()
                 load(v0_hbm, v0b, other, v_sem).start()
                 load(r_hbm, rbuf, other, r_sem).start()
+            pltpu.make_async_copy(w0_hbm, w0_ref, w_sem).wait()
+            w0 = w0_ref[...]
+            rows0 = w0.T.astype(BF)
             pltpu.make_async_copy(v0b, v0b, v_sem).wait()
             pltpu.make_async_copy(rbuf, rbuf, r_sem).wait()
         for k in range(nc):
@@ -412,9 +414,10 @@
         user_new, item_new = pl.pallas_call(
             functools.partial(kernel, ridge_u, ridge_i),
             out_shape=(pltpu.VMEM((rank, users), F32), pltpu.VMEM((rank, items), F32)),
-            in_specs=[any_space, any_space, vmem, any_space],
+            in_specs=[any_space, any_space, any_space, any_space],
             out_specs=(vmem, vmem),
             scratch_shapes=[
+                pltpu.VMEM((rank, users), F32),
                 pltpu.VMEM((4, users, blk), jnp.int32),
                 pltpu.VMEM((4, users, blk), F32),
                 pltpu.VMEM((4, rank, blk), F32),
@@ -426,7 +429,7 @@
                 pltpu.VMEM((4 * users, rank), BF),
                 pltpu.VMEM((rank, 4 * users), BF),
                 sums, sums, sums,
-                dma((4,)), dma, dma, dma, dma((4,)), dma, dma((2, 4)), dma, dma((4,)),
+                dma((4,)), dma, dma, dma, dma, dma((4,)), dma, dma((2, 4)), dma, dma((4,)),
                 dma, dma((4, CHUNKS)), dma((CHUNKS,)), dma,
                 pltpu.SemaphoreType.REGULAR, pltpu.SemaphoreType.REGULAR,
             ],

time: 104 us -> 104 us (level)
  no operation moved by 1% of the time
where the time goes in v6:
time: 104 us
  Pallas kernels  103 us (99%)
    pallas_call x1, Pallas kernels, local_step(): pl.pallas_call(functools.partial(kernel, ridge_u, ridge_i), out_shape=(pl...  102 us

profile of v6, /device:TPU:0, one launch (start us, length us, event | category | flops | bytes accessed | tf_op | source)
XLA Modules:
  0.0 103.6 jit_solution(12474539227206279233)
XLA Ops:
  0.6 101.6 %als_sweep.1 = (f32[64,128]{1,0:T(8,128)S(1)}, f32[64,8192]{1,0:T(8,128)S(1)}) custom-call(f32[128,8192]{1,0:T(8,128)} %r_hbm.1, s32[128,8192]{1,0:T(8,128)} %m_hbm.1, f32[64,128]{1,0:T(8,128)} %bitcast.5, f32[64,8192]{1,0:T(8,128)} %bitcast.4), custom_call_target="tpu_custom_call" | custom-call | tf_op jit(solution)/shard_map/als_sweep/pallas_call | solution.py:414
  102.2 1.3 %write_out.1 = (f32[64,128]{1,0:T(8,128)}, f32[64,8192]{1,0:T(8,128)}) custom-call(f32[64,128]{1,0:T(8,128)S(1)} %get-tuple-element.6.u_in, f32[64,8192]{1,0:T(8,128)S(1)} %get-tuple-element.7.v_in), custom_call_target="tpu_custom_call" | custom-call | tf_op jit(solution)/shard_map/write_out/pallas_call | solution.py:440

commit v7 on v6

--- a/solution.py
+++ b/solution.py
@@ -104,7 +104,7 @@
         return jnp.where(mint[s, :, cols] > 0, rbuf[s, :, cols] - scores, 0.0).astype(BF)
 
     def send_mask(s):
-        to_row(mown.at[s], mrecv.at[z], ms_sem, mr_sem.at[z], s).start()
+        to_row(mown.at[s], mrecv.at[z], ms_sem, mr_sem, s).start()
 
     first = jnp.zeros(w0_ref.shape[::-1], F32)
     for j, s in enumerate(order):
@@ -166,21 +166,15 @@
     def to_col(rnd, off):
         peer = lax.rem(c + off, 4)
         return pltpu.make_async_remote_copy(
-            src_ref=ar.at[rnd, c], dst_ref=ar.at[rnd, c], send_sem=as_sem, recv_sem=arr_sem.at[lax.rem(rnd, 2), c],
+            src_ref=ar.at[rnd, c], dst_ref=ar.at[rnd, c], send_sem=as_sem, recv_sem=arr_sem.at[lax.rem(rnd, 2)],
             device_id={"col": peer}, device_id_type=MESH)
-
-    def from_col(rnd, off):
-        peer = lax.rem(c + off, 4)
-        return pltpu.make_async_remote_copy(
-            src_ref=ar.at[rnd, peer], dst_ref=ar.at[rnd, peer], send_sem=as_sem,
-            recv_sem=arr_sem.at[lax.rem(rnd, 2), peer], device_id={"col": peer}, device_id_type=MESH)
 
     def sum_cols(rnd, x):
         ar[rnd, c] = x
         for off in range(1, 4):
             to_col(rnd, off).start()
-        for off in range(1, 4):
-            from_col(rnd, off).wait_recv()
+        others = ar.at[rnd, :3]
+        to_row(others, others, as_sem, arr_sem.at[lax.rem(rnd, 2)], z).wait_recv()
         return (ar[rnd, 0] + ar[rnd, 1]) + (ar[rnd, 2] + ar[rnd, 3])
 
     res = sum_cols(0, first.T) - ridge_u * w0
@@ -259,7 +253,8 @@
             def _():
                 give(peer, end).start()
 
-            to_row(mown.at[peer], mrecv.at[peer], ms_sem, mr_sem.at[peer], peer).wait_recv()
+        masks = mrecv.at[:3]
+        to_row(masks, masks, ms_sem, mr_sem, z).wait_recv()
         users = own_rows.shape[0]
         for s in range(4):
             wrow[s * users:(s + 1) * users] = wg[s].astype(F32).T.astype(BF)
@@ -288,6 +283,11 @@
 
     s0, s1, s2, s3 = (row_of(m) for m in range(4))
 
+    def sent_early():
+        sent(part, rs_sem, 3)
+        sent(mown, ms_sem, 3)
+        sent(ar.at[:, :3], as_sem, None)
+
     @pl.when(is_mid == 0)
     def _():
         inner = 1 + hi
@@ -305,10 +305,11 @@
 
         gather()
         each(own)
-        for s in (s1, s2, s3):
+        for s in (s1, s2):
             each(take(s))
+        sent_early()
+        each(take(s3))
         sent(wg, ws_sem, 1)
-        sent(part, rs_sem, 3)
         sent(vout.at[:, :blk], ag_sem, None)
 
     @pl.when(is_mid == 1)
@@ -378,12 +379,9 @@
         each(step)
         sent(wg, ws_sem, 4)
         sent(wg, ws_sem, 1)
-        sent(part, rs_sem, 3)
+        sent_early()
         for _ in range(5):
             sent(vout.at[:, :blk], ag_sem, None)
-
-    sent(mown, ms_sem, 3)
-    sent(ar.at[:, :3], as_sem, None)
 
 
 def finish_kernel(u_in, v_in, u_out, v_out, sem):
@@ -429,7 +427,7 @@
                 pltpu.VMEM((4 * users, rank), BF),
                 pltpu.VMEM((rank, 4 * users), BF),
                 sums, sums, sums,
-                dma((4,)), dma, dma, dma, dma, dma((4,)), dma, dma((2, 4)), dma, dma((4,)),
+                dma((4,)), dma, dma, dma, dma, dma, dma, dma((2,)), dma, dma((4,)),
                 dma, dma((4, CHUNKS)), dma((CHUNKS,)), dma,
                 pltpu.SemaphoreType.REGULAR, pltpu.SemaphoreType.REGULAR,
             ],

time: 104 us -> 104 us (level)
  no operation moved by 1% of the time
where the time goes in v7:
time: 104 us; the launch traced here: 103 us
  Pallas kernels  103 us (99%)
    pallas_call x1, Pallas kernels, local_step(): pl.pallas_call(functools.partial(kernel, ridge_u, ridge_i), out_shape=(pl...  102 us

profile of v7, /device:TPU:0, one launch (start us, length us, event | category | flops | bytes accessed | tf_op | source)
XLA Modules:
  0.0 103.5 jit_solution(17175791860048340690)
XLA Ops:
  0.6 101.5 %als_sweep.1 = (f32[64,128]{1,0:T(8,128)S(1)}, f32[64,8192]{1,0:T(8,128)S(1)}) custom-call(f32[128,8192]{1,0:T(8,128)} %r_hbm.1, s32[128,8192]{1,0:T(8,128)} %m_hbm.1, f32[64,128]{1,0:T(8,128)} %bitcast.5, f32[64,8192]{1,0:T(8,128)} %bitcast.4), custom_call_target="tpu_custom_call" | custom-call | tf_op jit(solution)/shard_map/als_sweep/pallas_call | solution.py:412
  102.1 1.3 %write_out.1 = (f32[64,128]{1,0:T(8,128)}, f32[64,8192]{1,0:T(8,128)}) custom-call(f32[64,128]{1,0:T(8,128)S(1)} %get-tuple-element.6.u_in, f32[64,8192]{1,0:T(8,128)S(1)} %get-tuple-element.7.v_in), custom_call_target="tpu_custom_call" | custom-call | tf_op jit(solution)/shard_map/write_out/pallas_call | solution.py:438

commit v8 on v7

--- a/solution.py
+++ b/solution.py
@@ -108,7 +108,10 @@
 
     first = jnp.zeros(w0_ref.shape[::-1], F32)
     for j, s in enumerate(order):
-        load(m_hbm, mint, s, ld_sem.at[j]).wait()
+        if j == 0:
+            load(m_hbm, mint, s, ld_sem.at[0]).wait()
+        elif j == 1:
+            pltpu.make_async_copy(mint.at[:3], mint.at[:3], ld_sem.at[1]).wait()
         for k in range(nc):
             m = mint[s, :, k * width:(k + 1) * width].astype(F32).astype(BF)
             mown[s, k] = m
@@ -139,7 +142,7 @@
             pltpu.make_async_copy(w0_hbm, w0_ref, w_sem).start()
             for i, other in enumerate(order):
                 if i:
-                    load(m_hbm, mint, other, ld_sem.at[i]).start()
+                    load(m_hbm, mint, other, ld_sem.at[1]).start()
                 load(v0_hbm, v0b, other, v_sem).start()
                 load(r_hbm, rbuf, other, r_sem).start()
             pltpu.make_async_copy(w0_hbm, w0_ref, w_sem).wait()
@@ -427,7 +430,7 @@
                 pltpu.VMEM((4 * users, rank), BF),
                 pltpu.VMEM((rank, 4 * users), BF),
                 sums, sums, sums,
-                dma((4,)), dma, dma, dma, dma, dma, dma, dma((2,)), dma, dma((4,)),
+                dma((2,)), dma, dma, dma, dma, dma, dma, dma((2,)), dma, dma((4,)),
                 dma, dma((4, CHUNKS)), dma((CHUNKS,)), dma,
                 pltpu.SemaphoreType.REGULAR, pltpu.SemaphoreType.REGULAR,
             ],

time: 104 us -> 104 us (level)
  no operation moved by 1% of the time
where the time goes in v8:
time: 104 us; the launch traced here: 103 us
  Pallas kernels  103 us (99%)
    pallas_call x1, Pallas kernels, local_step(): pl.pallas_call(functools.partial(kernel, ridge_u, ridge_i), out_shape=(pl...  101 us

profile of v8, /device:TPU:0, one launch (start us, length us, event | category | flops | bytes accessed | tf_op | source)
XLA Modules:
  0.0 103.5 jit_solution(5548037994332045362)
XLA Ops:
  0.6 101.5 %als_sweep.1 = (f32[64,128]{1,0:T(8,128)S(1)}, f32[64,8192]{1,0:T(8,128)S(1)}) custom-call(f32[128,8192]{1,0:T(8,128)} %r_hbm.1, s32[128,8192]{1,0:T(8,128)} %m_hbm.1, f32[64,128]{1,0:T(8,128)} %bitcast.5, f32[64,8192]{1,0:T(8,128)} %bitcast.4), custom_call_target="tpu_custom_call" | custom-call | tf_op jit(solution)/shard_map/als_sweep/pallas_call | solution.py:415
  102.1 1.3 %write_out.1 = (f32[64,128]{1,0:T(8,128)}, f32[64,8192]{1,0:T(8,128)}) custom-call(f32[64,128]{1,0:T(8,128)S(1)} %get-tuple-element.6.u_in, f32[64,8192]{1,0:T(8,128)S(1)} %get-tuple-element.7.v_in), custom_call_target="tpu_custom_call" | custom-call | tf_op jit(solution)/shard_map/write_out/pallas_call | solution.py:441
